TPU v7x, 256 devices: a whole 4x4x8 slice. The times are simulated.
256 devices in a mesh: tm: 8 (over x, core), space: 32 (over z, y).
Axes of the slice: x: 4, y: 4, z: 8, core: 2. Of those that a mesh axis runs over, the one named last changes fastest.
Arguments:
- initial_state: float32 [512, 3, 512], P('space'), may hold values from -1 to 1, as said below
- applied_field: float32 [512, 3, 512], P('space'), may hold values from -2 to 2
- coupling: float32 [512, 512], P('space'), may hold values from 0.5 to 2
Outputs:
- slice_states: float32 [8, 512, 3, 512], P('tm', 'space')
Inputs may be any that keep to these rules, and one draw needn't show every extreme that they name: `initial_state`: every cell's three components form a vector of length one.
All inputs are finite; a program needn't handle non-finite values.
Results may differ from a plain program's by a relative error of at most 0.00014.
Values sent between devices are 32-bit elements; how exact they have to be, the bound alone decides.
A program may use at most 128 MiB of HBM per device.

v0:
```python
import math

import jax
import jax.numpy as jnp
from jax import lax
from jax.sharding import Mesh
from jax.sharding import PartitionSpec as P

FINE = 2
TM = ("tm_0", "tm_1")


step_time = 0.06
damping = 0.02
stiffness = 0.25
thickness = 8.0


def with_halo(x, sides, width):
    for axis, dim in sides:
        peers, length = (lax.axis_size(axis), x.shape[dim])
        up = [(i, (i + 1) % peers) for i in range(peers - 1)]
        down = [(j, i) for i, j in up]
        last = lax.slice_in_dim(x, length - width, length, axis=dim)
        initial = lax.slice_in_dim(x, 0, width, axis=dim)
        before = lax.ppermute(last, axis, up)
        after = lax.ppermute(initial, axis, down)
        x = jnp.concatenate([before, x, after], axis=dim)
    return x


def laid_out(parts, dim):
    shape = list(parts.shape[1:])
    shape[dim] *= parts.shape[0]
    return jnp.moveaxis(parts, 0, dim).reshape(shape)


def all_blocks(x, axes, order):
    parts = x
    for k in order:
        parts = lax.all_gather(parts, axes[k])
    done = order[::-1]
    back = [done.index(k) for k in range(len(axes))]
    parts = parts.transpose(*back, *range(len(axes), parts.ndim))
    return parts.reshape(-1, *x.shape)


def gather_axes(x, axes, order, dim):
    return laid_out(all_blocks(x, axes, order), dim)


def spectral_tensor(row_index, column_index, length):
    half_length = length // 2
    signed_rows = jnp.where(row_index < half_length, row_index, row_index - length).astype(
        jnp.float32
    )
    signed_columns = jnp.where(
        column_index < half_length, column_index, column_index - length
    ).astype(jnp.float32)
    wave_rows = 2.0 * math.pi / length * signed_rows[:, None]
    wave_columns = 2.0 * math.pi / length * signed_columns[None, :]
    squared = wave_rows * wave_rows + wave_columns * wave_columns
    nonzero = squared > 0.0
    safe_square = jnp.where(nonzero, squared, 1.0)
    scaled_wave = jnp.sqrt(safe_square) * thickness
    film_factor = jnp.where(nonzero, (1.0 - jnp.exp(-scaled_wave)) / scaled_wave, 1.0)
    in_plane = (1.0 - film_factor) / safe_square
    nyquist = (row_index[:, None] == half_length) | (column_index[None, :] == half_length)
    normalizer = -1.0 / (length * length)
    tensor_first = in_plane * wave_columns * wave_columns * normalizer
    tensor_second = in_plane * wave_rows * wave_rows * normalizer
    tensor_cross = jnp.where(nyquist, 0.0, in_plane * wave_columns * wave_rows) * normalizer
    tensor_normal = film_factor * normalizer
    return (tensor_first, tensor_second, tensor_cross, tensor_normal)


def exchange_field(padded_state, padded_coupling):
    center_state = padded_state[1:-1]
    center_coupling = padded_coupling[1:-1]
    wide_state = jnp.pad(padded_state, ((0, 0), (0, 0), (1, 1)))
    wide_coupling = jnp.pad(padded_coupling, ((0, 0), (1, 1)))
    neighbour_sum = padded_coupling[2:, None, :] * (padded_state[2:] - center_state)
    neighbour_sum = neighbour_sum + padded_coupling[:-2, None, :] * (
        padded_state[:-2] - center_state
    )
    neighbour_sum = neighbour_sum + wide_coupling[1:-1, None, 2:] * (
        wide_state[1:-1, :, 2:] - center_state
    )
    neighbour_sum = neighbour_sum + wide_coupling[1:-1, None, :-2] * (
        wide_state[1:-1, :, :-2] - center_state
    )
    return stiffness * center_coupling[:, None, :] * neighbour_sum


def torque(magnet, effective):
    first_cross = jnp.cross(magnet, effective, axis=1)
    second_cross = jnp.cross(magnet, first_cross, axis=1)
    return -(first_cross + damping * second_cross) / (1.0 + damping * damping)


def phase_table(row_count, column_count, period, direction):
    row_ids = lax.broadcasted_iota(jnp.int32, (row_count, column_count), 0)
    column_ids = lax.broadcasted_iota(jnp.int32, (row_count, column_count), 1)
    angles = (row_ids * column_ids % period).astype(jnp.float32) * (2.0 * math.pi / period)
    return (jnp.cos(angles), direction * jnp.sin(angles))


def joined_table(row_count, column_count, period, direction):
    table_cos, table_sin = phase_table(row_count, column_count, period, direction)
    return jnp.concatenate([table_cos, table_sin], axis=1)


def contract(pattern, left, right):
    return jnp.einsum(pattern, left, right, precision=lax.Precision.HIGHEST)


def complex_apply(pattern, real_part, imag_part, joined):
    half_width = joined.shape[-1] // 2
    real_both = contract(pattern, real_part, joined)
    imag_both = contract(pattern, imag_part, joined)
    return (
        real_both[..., :half_width] - imag_both[..., half_width:],
        real_both[..., half_width:] + imag_both[..., :half_width],
    )


def apply_tensor(real_part, imag_part, tensor):
    tensor_first, tensor_second, tensor_cross, tensor_normal = tensor

    def mix_components(values):
        return jnp.stack(
            [
                tensor_first * values[0] + tensor_cross * values[1],
                tensor_cross * values[0] + tensor_second * values[1],
                tensor_normal * values[2],
            ],
            axis=0,
        )

    return (mix_components(real_part), mix_components(imag_part))


def shards(initial_state, applied_field, coupling):
    row_count, component_count, grid_size = initial_state.shape
    length = 2 * grid_size
    space_count = lax.axis_size("space")
    space_index = lax.axis_index("space")
    slice_count = lax.axis_size(TM)
    slice_index = lax.axis_index(TM)
    padded_coupling = with_halo(coupling, (("space", 0),), 1)
    index_all = jnp.arange(length, dtype=jnp.int32)
    local_demag = jnp.array([0.0, 0.0, -1.0], dtype=jnp.float32).reshape(1, 3, 1)
    forward_y = joined_table(grid_size, length, length, -1.0)
    inverse_y = joined_table(length, grid_size, length, 1.0)

    def transform_columns(real_part, imag_part):
        return complex_apply("yca,yk->cak", real_part, imag_part, forward_y)

    column_width = length // space_count
    columns = space_index * column_width + jnp.arange(column_width, dtype=jnp.int32)
    tensor = tuple((part_table.T for part_table in spectral_tensor(index_all, columns, length)))
    forward_x = joined_table(grid_size, length, length, -1.0)
    inverse_x_cos, inverse_x_sin = phase_table(length, grid_size, length, 1.0)

    def demag_field(magnet):
        both_parts = contract("rcx,xk->rck", magnet, forward_x)
        real_part = both_parts[..., :length]
        imag_part = both_parts[..., length:]
        real_part, imag_part = (
            lax.all_to_all(real_part, "space", split_axis=2, concat_axis=0, tiled=True),
            lax.all_to_all(imag_part, "space", split_axis=2, concat_axis=0, tiled=True),
        )
        real_part, imag_part = transform_columns(real_part, imag_part)
        real_part, imag_part = apply_tensor(real_part, imag_part, tensor)
        real_part, imag_part = complex_apply("cak,ky->cay", real_part, imag_part, inverse_y)
        real_part, imag_part = (
            lax.all_to_all(real_part, "space", split_axis=2, concat_axis=1, tiled=True),
            lax.all_to_all(imag_part, "space", split_axis=2, concat_axis=1, tiled=True),
        )
        return contract("cxr,xo->rco", real_part, inverse_x_cos) - contract(
            "cxr,xo->rco", imag_part, inverse_x_sin
        )

    def effective_fine(state_now):
        padded_state = with_halo(state_now, (("space", 0),), 1)
        return (
            exchange_field(padded_state, padded_coupling) + demag_field(state_now) + applied_field
        )

    def propagate_coarse(magnet):
        padded_state = with_halo(magnet, (("space", 0),), 1)
        effective = (
            exchange_field(padded_state, padded_coupling) + applied_field + magnet * local_demag
        )
        return magnet + FINE * step_time * torque(magnet, effective)

    def coarse_sweep(jump_table):

        def one_turn(turn_index, loop_state):
            current, start_state, coarse_end, slice_end = loop_state
            predicted = propagate_coarse(current)
            advanced = predicted
            if jump_table is not None:
                advanced = predicted + lax.dynamic_index_in_dim(
                    jump_table, turn_index, 0, keepdims=False
                )
            is_mine = turn_index == slice_index
            return (
                advanced,
                jnp.where(is_mine, current, start_state),
                jnp.where(is_mine, predicted, coarse_end),
                jnp.where(is_mine, advanced, slice_end),
            )

        finished = lax.fori_loop(
            0, slice_count, one_turn, (initial_state, initial_state, initial_state, initial_state)
        )
        return (finished[1], finished[2], finished[3])

    start_state, coarse_end, slice_end = coarse_sweep(None)
    magnet = start_state
    for repeat in range(FINE):
        first_rate = torque(magnet, effective_fine(magnet))
        predicted = magnet + step_time * first_rate
        second_rate = torque(predicted, effective_fine(predicted))
        magnet = magnet + 0.5 * step_time * (first_rate + second_rate)
    jump_term = magnet - coarse_end
    jump_table = gather_axes(jump_term[None], ("tm_0", "tm_1"), (0, 1), 0)
    start_state, coarse_end, slice_end = coarse_sweep(jump_table)
    return slice_end[None]


def solution(mesh):
    split = Mesh(mesh.devices.reshape(4, 2, mesh.shape["space"]), ("tm_0", "tm_1", "space"))
    return jax.shard_map(
        shards,
        mesh=split,
        in_specs=(P("space", None, None), P("space", None, None), P("space", None)),
        out_specs=P(TM, "space", None, None),
        check_vma=False,
    )
```

profile of v0, /device:TPU:128, one launch (start us, length us, event | category | flops | bytes accessed | tf_op | source)
XLA Modules:
  0.0 759.5 jit_solution(11310628621887339754)
XLA Ops:
  5.2 5.8 collective-permute-start.5
  11.0 9.1 %sine_multiply_fusion = (f32[512,1024]{1,0:T(8,128)S(1)}, f32[512,1024]{1,0:T(8,128)}) fusion(), kind=kLoop, calls=%fused_computation.98 | loop fusion | flops 7864320 | bytes 4194304 | tf_op jit(solution)/shard_map/mul | solution.py:105
  20.2 89.8 %while.38 = (s32[]{:T(128)}, f32[16,3,512]{2,0,1:T(8,128)S(1)}, f32[16,3,512]{2,0,1:T(8,128)S(1)}, f32[16,3,512]{2,0,1:T(8,128)S(1)}, f32[16,512]{1,0:T(8,128)S(...) while((s32[]{:T(128)}, f32[16,3,512]{2,0,1:T(8,128)S(1)}, ...), condition=%wide.region_1.3_spmd.clone, body=%wide.region_0.2_spmd.clone.sunk | while | flops 1114979 | bytes 2847356 | solution.py:215
  26.2 4.8 collective-permute-done.1
  37.4 4.8 collective-permute-done.1
  48.6 4.8 collective-permute-done.1
  59.8 4.8 collective-permute-done.1
  71.0 4.8 collective-permute-done.1
  82.3 4.8 collective-permute-done.1
  93.5 4.8 collective-permute-done.1
  104.7 4.8 collective-permute-done.1
  119.0 7.4 all-to-all-start
  126.5 9.2 %fusion.58 = (f32[1024,512]{1,0:T(8,128)}, f32[1024,512]{1,0:T(8,128)}) fusion(), kind=kLoop, calls=%fused_computation.106 | loop fusion | flops 7340032 | bytes 4194304 | tf_op jit(solution)/shard_map/sin | solution.py:105
  140.5 10.5 %all-to-all-start.1 = ((f32[32,1,1536]{2,1,0:T(1,128)}), f32[32,1,1536]{2,1,0:T(1,128)}, u32[]{:S(2)}, u32[]{:S(2)}) async-start(f32[32,1,1536]{2,1,0:T(1,128)} %reshape.1551), calls=%async_computation.1 | async-start | bytes 393216 | tf_op jit(solution)/shard_map/all_to_all | solution.py:171
  185.6 9.8 %all-to-all-start.3 = ((f32[32,1,1536]{2,1,0:T(1,128)}), f32[32,1,1536]{2,1,0:T(1,128)S(1)}, u32[]{:S(2)}, u32[]{:S(2)}) async-start(f32[32,1,1536]{2,1,0:T(1,128)} %reshape.1557), calls=%async_computation.3 | async-start | bytes 393216 | tf_op jit(solution)/shard_map/all_to_all | solution.py:178
  205.9 11.4 %all-to-all-start.2 = ((f32[32,1,1536]{2,1,0:T(1,128)}), f32[32,1,1536]{2,1,0:T(1,128)}, u32[]{:S(2)}, u32[]{:S(2)}) async-start(f32[32,1,1536]{2,1,0:T(1,128)} %reshape.1555), calls=%async_computation.2 | async-start | bytes 393216 | tf_op jit(solution)/shard_map/all_to_all | solution.py:177
  223.4 10.7 %fusion.74 = f32[512,48]{0,1} fusion(f32[1024,48]{0,1:T(8,128)} %bitcast.551), kind=kOutput, calls=%fused_computation.115 | convolution fusion | flops 309329920 | bytes 294912
  240.3 10.7 %fusion.66 = f32[512,48]{0,1:S(1)} fusion(f32[1024,48]{0,1:T(8,128)} %bitcast.552), kind=kOutput, calls=%fused_computation.111 | convolution fusion | flops 309329920 | bytes 294912
  260.4 9.8 %all-to-all-start.4 = ((f32[32,1,1536]{2,1,0:T(1,128)}), f32[32,1,1536]{2,1,0:T(1,128)S(1)}, u32[]{:S(2)}, u32[]{:S(2)}) async-start(f32[32,1,1536]{2,1,0:T(1,128)} %reshape.1561), calls=%async_computation.4 | async-start | bytes 393216 | tf_op jit(solution)/shard_map/all_to_all | solution.py:170
  278.3 8.7 %all-to-all-start.5 = ((f32[32,1,1536]{2,1,0:T(1,128)}), f32[32,1,1536]{2,1,0:T(1,128)}, u32[]{:S(2)}, u32[]{:S(2)}) async-start(f32[32,1,1536]{2,1,0:T(1,128)} %reshape.1559), calls=%async_computation.5 | async-start | bytes 393216 | tf_op jit(solution)/shard_map/all_to_all | solution.py:171
  322.7 9.8 %all-to-all-start.7 = ((f32[32,1,1536]{2,1,0:T(1,128)}), f32[32,1,1536]{2,1,0:T(1,128)S(1)}, u32[]{:S(2)}, u32[]{:S(2)}) async-start(f32[32,1,1536]{2,1,0:T(1,128)} %reshape.1565), calls=%async_computation.7 | async-start | bytes 393216 | tf_op jit(solution)/shard_map/all_to_all | solution.py:178
  332.5 4.6 collective-permute-start.8
  343.6 11.4 %all-to-all-start.6 = ((f32[32,1,1536]{2,1,0:T(1,128)}), f32[32,1,1536]{2,1,0:T(1,128)}, u32[]{:S(2)}, u32[]{:S(2)}) async-start(f32[32,1,1536]{2,1,0:T(1,128)} %reshape.1563), calls=%async_computation.6 | async-start | bytes 393216 | tf_op jit(solution)/shard_map/all_to_all | solution.py:177
  362.2 10.7 %fusion.72 = f32[512,48]{0,1} fusion(f32[1024,48]{0,1:T(8,128)} %bitcast.553), kind=kOutput, calls=%fused_computation.114 | convolution fusion | flops 309329920 | bytes 294912
  379.2 10.5 %fusion.64 = f32[512,48]{0,1:S(1)} fusion(f32[1024,48]{0,1:T(8,128)} %bitcast.554), kind=kOutput, calls=%fused_computation.110 | convolution fusion | flops 309329920 | bytes 294912
  400.4 9.8 %all-to-all-start.8 = ((f32[32,1,1536]{2,1,0:T(1,128)}), f32[32,1,1536]{2,1,0:T(1,128)S(1)}, u32[]{:S(2)}, u32[]{:S(2)}) async-start(f32[32,1,1536]{2,1,0:T(1,128)} %reshape.1569), calls=%async_computation.8 | async-start | bytes 393216 | tf_op jit(solution)/shard_map/all_to_all | solution.py:170
  416.7 8.9 %all-to-all-start.9 = ((f32[32,1,1536]{2,1,0:T(1,128)}), f32[32,1,1536]{2,1,0:T(1,128)}, u32[]{:S(2)}, u32[]{:S(2)}) async-start(f32[32,1,1536]{2,1,0:T(1,128)} %reshape.1567), calls=%async_computation.9 | async-start | bytes 393216 | tf_op jit(solution)/shard_map/all_to_all | solution.py:171
  461.5 9.8 %all-to-all-start.11 = ((f32[32,1,1536]{2,1,0:T(1,128)}), f32[32,1,1536]{2,1,0:T(1,128)S(1)}, u32[]{:S(2)}, u32[]{:S(2)}) async-start(f32[32,1,1536]{2,1,0:T(1,128)} %reshape.1573), calls=%async_computation.11 | async-start | bytes 393216 | tf_op jit(solution)/shard_map/all_to_all | solution.py:178
  482.5 11.4 %all-to-all-start.10 = ((f32[32,1,1536]{2,1,0:T(1,128)}), f32[32,1,1536]{2,1,0:T(1,128)}, u32[]{:S(2)}, u32[]{:S(2)}) async-start(f32[32,1,1536]{2,1,0:T(1,128)} %reshape.1571), calls=%async_computation.10 | async-start | bytes 393216 | tf_op jit(solution)/shard_map/all_to_all | solution.py:177
  500.0 10.7 %fusion.70 = f32[512,48]{0,1} fusion(f32[1024,48]{0,1:T(8,128)} %bitcast.555), kind=kOutput, calls=%fused_computation.113 | convolution fusion | flops 309329920 | bytes 294912
  517.0 10.5 %fusion.62 = f32[512,48]{0,1:S(1)} fusion(f32[1024,48]{0,1:T(8,128)} %bitcast.556), kind=kOutput, calls=%fused_computation.109 | convolution fusion | flops 309329920 | bytes 294912
  538.2 9.8 %all-to-all-start.12 = ((f32[32,1,1536]{2,1,0:T(1,128)}), f32[32,1,1536]{2,1,0:T(1,128)S(1)}, u32[]{:S(2)}, u32[]{:S(2)}) async-start(f32[32,1,1536]{2,1,0:T(1,128)} %reshape.1577), calls=%async_computation.12 | async-start | bytes 393216 | tf_op jit(solution)/shard_map/all_to_all | solution.py:170
  554.6 8.9 %all-to-all-start.13 = ((f32[32,1,1536]{2,1,0:T(1,128)}), f32[32,1,1536]{2,1,0:T(1,128)}, u32[]{:S(2)}, u32[]{:S(2)}) async-start(f32[32,1,1536]{2,1,0:T(1,128)} %reshape.1575), calls=%async_computation.13 | async-start | bytes 393216 | tf_op jit(solution)/shard_map/all_to_all | solution.py:171
  595.6 9.8 %all-to-all-start.15 = ((f32[32,1,1536]{2,1,0:T(1,128)}), f32[32,1,1536]{2,1,0:T(1,128)S(1)}, u32[]{:S(2)}, u32[]{:S(2)}) async-start(f32[32,1,1536]{2,1,0:T(1,128)} %reshape.1581), calls=%async_computation.15 | async-start | bytes 393216 | tf_op jit(solution)/shard_map/all_to_all | solution.py:178
  613.9 11.4 %all-to-all-start.14 = ((f32[32,1,1536]{2,1,0:T(1,128)}), f32[32,1,1536]{2,1,0:T(1,128)}, u32[]{:S(2)}, u32[]{:S(2)}) async-start(f32[32,1,1536]{2,1,0:T(1,128)} %reshape.1579), calls=%async_computation.14 | async-start | bytes 393216 | tf_op jit(solution)/shard_map/all_to_all | solution.py:177
  627.8 9.8 %fusion.68 = f32[512,48]{0,1} fusion(f32[1024,48]{0,1:T(8,128)S(1)} %bitcast.557), kind=kOutput, calls=%fused_computation.112 | convolution fusion | flops 309329920 | bytes 294912
  641.0 9.4 %fusion.60 = f32[512,48]{0,1:S(1)} fusion(f32[1024,48]{0,1:T(8,128)S(1)} %bitcast.558), kind=kOutput, calls=%fused_computation.108 | convolution fusion | flops 309329920 | bytes 294912
  650.9 12.9 %all-gather = f32[64,3,512]{2,0,1:T(8,128)S(1)} all-gather(f32[16,3,512]{2,0,1:T(8,128)S(1)} %fusion.203), channel_id=2, replica_groups=mesh['tm_0'=4,'tm_1'=2,'space'=32] {'tm_0'}, dimensions={0}, use_global_device_ids=true | all-gather | bytes 491520 | tf_op jit(solution)/shard_map/all_gather | solution.py:41
  666.2 92.4 %while.39 = (s32[]{:T(128)}, f32[16,3,512]{2,0,1:T(8,128)S(1)}, f32[16,3,512]{2,0,1:T(8,128)S(1)}, f32[16,512]{1,0:T(8,128)S(1)}, f32[18,512]{1,0:T(8,128)S(1)},...) while((s32[]{:T(128)}, f32[16,3,512]{2,0,1:T(8,128)S(1)}, ...), condition=%wide.region_3.5_spmd.clone, body=%wide.region_2.4_spmd.clone.sunk | while | flops 1114979 | bytes 2749063 | solution.py:215
  666.2 4.6 collective-permute-start.2
  672.8 6.8 collective-permute-done.3
  686.1 4.8 collective-permute-done.3
  697.3 4.8 collective-permute-done.3
  708.5 4.8 collective-permute-done.3
  719.7 4.8 collective-permute-done.3
  730.9 4.8 collective-permute-done.3
  742.2 4.8 collective-permute-done.3
  753.4 4.8 collective-permute-done.3
  (653 shorter events, 388.5 us)
Async XLA Ops:
  1.6 18.5 %collective-permute-start.4 = (f32[1,512]{1,0:T(1,128)S(1)}, f32[1,512]{1,0:T(1,128)S(1)}, u32[]{:S(2)}, u32[]{:S(2)}) collective-permute-start(f32[1,512]{1,0:T(1,128)S(1)} %get-tuple-element.637), channel_id=1, source_target_pairs={{0,1},{1,2},{2,3},{3,4},{4,5},{5,6},{6,7},{7,8},{8,9},{9,10},{10,1... | collective-permute-start | bytes 6152 | tf_op jit(solution)/shard_map/ppermute | solution.py:26
  5.2 14.9 %collective-permute-start.5 = (f32[1,512]{1,0:T(1,128)S(1)}, f32[1,512]{1,0:T(1,128)S(1)}, u32[]{:S(2)}, u32[]{:S(2)}) collective-permute-start(f32[1,512]{1,0:T(1,128)S(1)} %get-tuple-element.638), channel_id=1, source_target_pairs={{1,0},{2,1},{3,2},{4,3},{5,4},{6,5},{7,6},{8,7},{9,8},{10,9},{11,1... | collective-permute-start | bytes 6152 | tf_op jit(solution)/shard_map/ppermute | solution.py:27
  20.2 6.0 collective-permute-start
  22.1 8.8 %collective-permute-start.1 = (f32[1,3,512]{2,0,1:T(1,128)S(1)}, f32[1,3,512]{2,0,1:T(1,128)S(1)}, u32[]{:S(2)}, u32[]{:S(2)}) collective-permute-start(f32[1,3,512]{2,0,1:T(1,128)S(1)} %get-tuple-element.785), channel_id=1, source_target_pairs={{0,1},{1,2},{2,3},{3,4},{4,5},{5,6},{6,7},{7,8},{8,9},{9,10},{10,1... | collective-permute-start | bytes 18440 | tf_op jit(solution)/shard_map/while/body/eval_jaxpr/ppermute | solution.py:26
  31.4 6.0 collective-permute-start
  33.3 8.8 %collective-permute-start.1 = (f32[1,3,512]{2,0,1:T(1,128)S(1)}, f32[1,3,512]{2,0,1:T(1,128)S(1)}, u32[]{:S(2)}, u32[]{:S(2)}) collective-permute-start(f32[1,3,512]{2,0,1:T(1,128)S(1)} %get-tuple-element.785), channel_id=1, source_target_pairs={{0,1},{1,2},{2,3},{3,4},{4,5},{5,6},{6,7},{7,8},{8,9},{9,10},{10,1... | collective-permute-start | bytes 18440 | tf_op jit(solution)/shard_map/while/body/eval_jaxpr/ppermute | solution.py:26
  42.6 6.0 collective-permute-start
  44.6 8.8 %collective-permute-start.1 = (f32[1,3,512]{2,0,1:T(1,128)S(1)}, f32[1,3,512]{2,0,1:T(1,128)S(1)}, u32[]{:S(2)}, u32[]{:S(2)}) collective-permute-start(f32[1,3,512]{2,0,1:T(1,128)S(1)} %get-tuple-element.785), channel_id=1, source_target_pairs={{0,1},{1,2},{2,3},{3,4},{4,5},{5,6},{6,7},{7,8},{8,9},{9,10},{10,1... | collective-permute-start | bytes 18440 | tf_op jit(solution)/shard_map/while/body/eval_jaxpr/ppermute | solution.py:26
  53.9 6.0 collective-permute-start
  55.8 8.8 %collective-permute-start.1 = (f32[1,3,512]{2,0,1:T(1,128)S(1)}, f32[1,3,512]{2,0,1:T(1,128)S(1)}, u32[]{:S(2)}, u32[]{:S(2)}) collective-permute-start(f32[1,3,512]{2,0,1:T(1,128)S(1)} %get-tuple-element.785), channel_id=1, source_target_pairs={{0,1},{1,2},{2,3},{3,4},{4,5},{5,6},{6,7},{7,8},{8,9},{9,10},{10,1... | collective-permute-start | bytes 18440 | tf_op jit(solution)/shard_map/while/body/eval_jaxpr/ppermute | solution.py:26
  65.1 6.0 collective-permute-start
  67.0 8.8 %collective-permute-start.1 = (f32[1,3,512]{2,0,1:T(1,128)S(1)}, f32[1,3,512]{2,0,1:T(1,128)S(1)}, u32[]{:S(2)}, u32[]{:S(2)}) collective-permute-start(f32[1,3,512]{2,0,1:T(1,128)S(1)} %get-tuple-element.785), channel_id=1, source_target_pairs={{0,1},{1,2},{2,3},{3,4},{4,5},{5,6},{6,7},{7,8},{8,9},{9,10},{10,1... | collective-permute-start | bytes 18440 | tf_op jit(solution)/shard_map/while/body/eval_jaxpr/ppermute | solution.py:26
  78.2 8.8 %collective-permute-start.1 = (f32[1,3,512]{2,0,1:T(1,128)S(1)}, f32[1,3,512]{2,0,1:T(1,128)S(1)}, u32[]{:S(2)}, u32[]{:S(2)}) collective-permute-start(f32[1,3,512]{2,0,1:T(1,128)S(1)} %get-tuple-element.785), channel_id=1, source_target_pairs={{0,1},{1,2},{2,3},{3,4},{4,5},{5,6},{6,7},{7,8},{8,9},{9,10},{10,1... | collective-permute-start | bytes 18440 | tf_op jit(solution)/shard_map/while/body/eval_jaxpr/ppermute | solution.py:26
  89.4 8.8 %collective-permute-start.1 = (f32[1,3,512]{2,0,1:T(1,128)S(1)}, f32[1,3,512]{2,0,1:T(1,128)S(1)}, u32[]{:S(2)}, u32[]{:S(2)}) collective-permute-start(f32[1,3,512]{2,0,1:T(1,128)S(1)} %get-tuple-element.785), channel_id=1, source_target_pairs={{0,1},{1,2},{2,3},{3,4},{4,5},{5,6},{6,7},{7,8},{8,9},{9,10},{10,1... | collective-permute-start | bytes 18440 | tf_op jit(solution)/shard_map/while/body/eval_jaxpr/ppermute | solution.py:26
  100.7 8.8 %collective-permute-start.1 = (f32[1,3,512]{2,0,1:T(1,128)S(1)}, f32[1,3,512]{2,0,1:T(1,128)S(1)}, u32[]{:S(2)}, u32[]{:S(2)}) collective-permute-start(f32[1,3,512]{2,0,1:T(1,128)S(1)} %get-tuple-element.785), channel_id=1, source_target_pairs={{0,1},{1,2},{2,3},{3,4},{4,5},{5,6},{6,7},{7,8},{8,9},{9,10},{10,1... | collective-permute-start | bytes 18440 | tf_op jit(solution)/shard_map/while/body/eval_jaxpr/ppermute | solution.py:26
  119.0 21.4 %all-to-all-start = ((f32[32,1,1536]{2,1,0:T(1,128)}), f32[32,1,1536]{2,1,0:T(1,128)S(1)}, u32[]{:S(2)}, u32[]{:S(2)}) async-start(f32[32,1,1536]{2,1,0:T(1,128)} %reshape.1553), calls=%async_computation | async-start | bytes 393216 | tf_op jit(solution)/shard_map/all_to_all | solution.py:170
  140.5 21.4 %all-to-all-start.1 = ((f32[32,1,1536]{2,1,0:T(1,128)}), f32[32,1,1536]{2,1,0:T(1,128)}, u32[]{:S(2)}, u32[]{:S(2)}) async-start(f32[32,1,1536]{2,1,0:T(1,128)} %reshape.1551), calls=%async_computation.1 | async-start | bytes 393216 | tf_op jit(solution)/shard_map/all_to_all | solution.py:171
  185.6 20.4 %all-to-all-start.3 = ((f32[32,1,1536]{2,1,0:T(1,128)}), f32[32,1,1536]{2,1,0:T(1,128)S(1)}, u32[]{:S(2)}, u32[]{:S(2)}) async-start(f32[32,1,1536]{2,1,0:T(1,128)} %reshape.1557), calls=%async_computation.3 | async-start | bytes 393216 | tf_op jit(solution)/shard_map/all_to_all | solution.py:178
  195.4 21.9 %collective-permute-start.6 = (f32[1,3,512]{2,0,1:T(1,128)S(1)}, f32[1,3,512]{2,0,1:T(1,128)S(1)}, u32[]{:S(2)}, u32[]{:S(2)}) collective-permute-start(f32[1,3,512]{2,0,1:T(1,128)S(1)} %get-tuple-element.631), channel_id=1, source_target_pairs={{1,0},{2,1},{3,2},{4,3},{5,4},{6,5},{7,6},{8,7},{9,8},{10,9},{11,1... | collective-permute-start | bytes 18440 | tf_op jit(solution)/shard_map/ppermute | solution.py:27
  200.0 17.4 %collective-permute-start.7 = (f32[1,3,512]{2,0,1:T(1,128)S(1)}, f32[1,3,512]{2,0,1:T(1,128)S(1)}, u32[]{:S(2)}, u32[]{:S(2)}) collective-permute-start(f32[1,3,512]{2,0,1:T(1,128)S(1)} %get-tuple-element.630), channel_id=1, source_target_pairs={{0,1},{1,2},{2,3},{3,4},{4,5},{5,6},{6,7},{7,8},{8,9},{9,10},{10,1... | collective-permute-start | bytes 18440 | tf_op jit(solution)/shard_map/ppermute | solution.py:26
  205.9 28.2 %all-to-all-start.2 = ((f32[32,1,1536]{2,1,0:T(1,128)}), f32[32,1,1536]{2,1,0:T(1,128)}, u32[]{:S(2)}, u32[]{:S(2)}) async-start(f32[32,1,1536]{2,1,0:T(1,128)} %reshape.1555), calls=%async_computation.2 | async-start | bytes 393216 | tf_op jit(solution)/shard_map/all_to_all | solution.py:177
  260.4 17.8 %all-to-all-start.4 = ((f32[32,1,1536]{2,1,0:T(1,128)}), f32[32,1,1536]{2,1,0:T(1,128)S(1)}, u32[]{:S(2)}, u32[]{:S(2)}) async-start(f32[32,1,1536]{2,1,0:T(1,128)} %reshape.1561), calls=%async_computation.4 | async-start | bytes 393216 | tf_op jit(solution)/shard_map/all_to_all | solution.py:170
  278.3 19.0 %all-to-all-start.5 = ((f32[32,1,1536]{2,1,0:T(1,128)}), f32[32,1,1536]{2,1,0:T(1,128)}, u32[]{:S(2)}, u32[]{:S(2)}) async-start(f32[32,1,1536]{2,1,0:T(1,128)} %reshape.1559), calls=%async_computation.5 | async-start | bytes 393216 | tf_op jit(solution)/shard_map/all_to_all | solution.py:171
  322.7 20.9 %all-to-all-start.7 = ((f32[32,1,1536]{2,1,0:T(1,128)}), f32[32,1,1536]{2,1,0:T(1,128)S(1)}, u32[]{:S(2)}, u32[]{:S(2)}) async-start(f32[32,1,1536]{2,1,0:T(1,128)} %reshape.1565), calls=%async_computation.7 | async-start | bytes 393216 | tf_op jit(solution)/shard_map/all_to_all | solution.py:178
  332.5 22.4 %collective-permute-start.8 = (f32[1,3,512]{2,0,1:T(1,128)S(1)}, f32[1,3,512]{2,0,1:T(1,128)S(1)}, u32[]{:S(2)}, u32[]{:S(2)}) collective-permute-start(f32[1,3,512]{2,0,1:T(1,128)S(1)} %get-tuple-element.629), channel_id=1, source_target_pairs={{1,0},{2,1},{3,2},{4,3},{5,4},{6,5},{7,6},{8,7},{9,8},{10,9},{11,1... | collective-permute-start | bytes 18440 | tf_op jit(solution)/shard_map/ppermute | solution.py:27
  337.1 17.9 %collective-permute-start.9 = (f32[1,3,512]{2,0,1:T(1,128)S(1)}, f32[1,3,512]{2,0,1:T(1,128)S(1)}, u32[]{:S(2)}, u32[]{:S(2)}) collective-permute-start(f32[1,3,512]{2,0,1:T(1,128)S(1)} %get-tuple-element.628), channel_id=1, source_target_pairs={{0,1},{1,2},{2,3},{3,4},{4,5},{5,6},{6,7},{7,8},{8,9},{9,10},{10,1... | collective-permute-start | bytes 18440 | tf_op jit(solution)/shard_map/ppermute | solution.py:26
  343.6 29.3 %all-to-all-start.6 = ((f32[32,1,1536]{2,1,0:T(1,128)}), f32[32,1,1536]{2,1,0:T(1,128)}, u32[]{:S(2)}, u32[]{:S(2)}) async-start(f32[32,1,1536]{2,1,0:T(1,128)} %reshape.1563), calls=%async_computation.6 | async-start | bytes 393216 | tf_op jit(solution)/shard_map/all_to_all | solution.py:177
  400.4 16.4 %all-to-all-start.8 = ((f32[32,1,1536]{2,1,0:T(1,128)}), f32[32,1,1536]{2,1,0:T(1,128)S(1)}, u32[]{:S(2)}, u32[]{:S(2)}) async-start(f32[32,1,1536]{2,1,0:T(1,128)} %reshape.1569), calls=%async_computation.8 | async-start | bytes 393216 | tf_op jit(solution)/shard_map/all_to_all | solution.py:170
  416.7 19.2 %all-to-all-start.9 = ((f32[32,1,1536]{2,1,0:T(1,128)}), f32[32,1,1536]{2,1,0:T(1,128)}, u32[]{:S(2)}, u32[]{:S(2)}) async-start(f32[32,1,1536]{2,1,0:T(1,128)} %reshape.1567), calls=%async_computation.9 | async-start | bytes 393216 | tf_op jit(solution)/shard_map/all_to_all | solution.py:171
  461.5 21.0 %all-to-all-start.11 = ((f32[32,1,1536]{2,1,0:T(1,128)}), f32[32,1,1536]{2,1,0:T(1,128)S(1)}, u32[]{:S(2)}, u32[]{:S(2)}) async-start(f32[32,1,1536]{2,1,0:T(1,128)} %reshape.1573), calls=%async_computation.11 | async-start | bytes 393216 | tf_op jit(solution)/shard_map/all_to_all | solution.py:178
  471.4 22.5 %collective-permute-start.10 = (f32[1,3,512]{2,0,1:T(1,128)S(1)}, f32[1,3,512]{2,0,1:T(1,128)S(1)}, u32[]{:S(2)}, u32[]{:S(2)}) collective-permute-start(f32[1,3,512]{2,0,1:T(1,128)S(1)} %get-tuple-element.627), channel_id=1, source_target_pairs={{1,0},{2,1},{3,2},{4,3},{5,4},{6,5},{7,6},{8,7},{9,8},{10,9},{11,1... | collective-permute-start | bytes 18440 | tf_op jit(solution)/shard_map/ppermute | solution.py:27
  476.0 18.0 %collective-permute-start.11 = (f32[1,3,512]{2,0,1:T(1,128)S(1)}, f32[1,3,512]{2,0,1:T(1,128)S(1)}, u32[]{:S(2)}, u32[]{:S(2)}) collective-permute-start(f32[1,3,512]{2,0,1:T(1,128)S(1)} %get-tuple-element.626), channel_id=1, source_target_pairs={{0,1},{1,2},{2,3},{3,4},{4,5},{5,6},{6,7},{7,8},{8,9},{9,10},{10,1... | collective-permute-start | bytes 18440 | tf_op jit(solution)/shard_map/ppermute | solution.py:26
  482.5 28.2 %all-to-all-start.10 = ((f32[32,1,1536]{2,1,0:T(1,128)}), f32[32,1,1536]{2,1,0:T(1,128)}, u32[]{:S(2)}, u32[]{:S(2)}) async-start(f32[32,1,1536]{2,1,0:T(1,128)} %reshape.1571), calls=%async_computation.10 | async-start | bytes 393216 | tf_op jit(solution)/shard_map/all_to_all | solution.py:177
  538.2 16.4 %all-to-all-start.12 = ((f32[32,1,1536]{2,1,0:T(1,128)}), f32[32,1,1536]{2,1,0:T(1,128)S(1)}, u32[]{:S(2)}, u32[]{:S(2)}) async-start(f32[32,1,1536]{2,1,0:T(1,128)} %reshape.1577), calls=%async_computation.12 | async-start | bytes 393216 | tf_op jit(solution)/shard_map/all_to_all | solution.py:170
  554.6 19.3 %all-to-all-start.13 = ((f32[32,1,1536]{2,1,0:T(1,128)}), f32[32,1,1536]{2,1,0:T(1,128)}, u32[]{:S(2)}, u32[]{:S(2)}) async-start(f32[32,1,1536]{2,1,0:T(1,128)} %reshape.1575), calls=%async_computation.13 | async-start | bytes 393216 | tf_op jit(solution)/shard_map/all_to_all | solution.py:171
  595.6 18.3 %all-to-all-start.15 = ((f32[32,1,1536]{2,1,0:T(1,128)}), f32[32,1,1536]{2,1,0:T(1,128)S(1)}, u32[]{:S(2)}, u32[]{:S(2)}) async-start(f32[32,1,1536]{2,1,0:T(1,128)} %reshape.1581), calls=%async_computation.15 | async-start | bytes 393216 | tf_op jit(solution)/shard_map/all_to_all | solution.py:178
  605.4 19.9 %collective-permute-start.12 = (f32[1,3,512]{2,0,1:T(1,128)S(1)}, f32[1,3,512]{2,0,1:T(1,128)S(1)}, u32[]{:S(2)}, u32[]{:S(2)}) collective-permute-start(f32[1,3,512]{2,0,1:T(1,128)S(1)} %get-tuple-element.625), channel_id=1, source_target_pairs={{1,0},{2,1},{3,2},{4,3},{5,4},{6,5},{7,6},{8,7},{9,8},{10,9},{11,1... | collective-permute-start | bytes 18440 | tf_op jit(solution)/shard_map/ppermute | solution.py:27
  610.0 15.3 %collective-permute-start.13 = (f32[1,3,512]{2,0,1:T(1,128)S(1)}, f32[1,3,512]{2,0,1:T(1,128)S(1)}, u32[]{:S(2)}, u32[]{:S(2)}) collective-permute-start(f32[1,3,512]{2,0,1:T(1,128)S(1)} %get-tuple-element.624), channel_id=1, source_target_pairs={{0,1},{1,2},{2,3},{3,4},{4,5},{5,6},{6,7},{7,8},{8,9},{9,10},{10,1... | collective-permute-start | bytes 18440 | tf_op jit(solution)/shard_map/ppermute | solution.py:26
  613.9 23.7 %all-to-all-start.14 = ((f32[32,1,1536]{2,1,0:T(1,128)}), f32[32,1,1536]{2,1,0:T(1,128)}, u32[]{:S(2)}, u32[]{:S(2)}) async-start(f32[32,1,1536]{2,1,0:T(1,128)} %reshape.1579), calls=%async_computation.14 | async-start | bytes 393216 | tf_op jit(solution)/shard_map/all_to_all | solution.py:177
  666.2 6.6 collective-permute-start.2
  670.8 8.8 %collective-permute-start.3 = (f32[1,3,512]{2,0,1:T(1,128)S(1)}, f32[1,3,512]{2,0,1:T(1,128)S(1)}, u32[]{:S(2)}, u32[]{:S(2)}) collective-permute-start(f32[1,3,512]{2,0,1:T(1,128)S(1)} %get-tuple-element.810), channel_id=1, source_target_pairs={{0,1},{1,2},{2,3},{3,4},{4,5},{5,6},{6,7},{7,8},{8,9},{9,10},{10,1... | collective-permute-start | bytes 18440 | tf_op jit(solution)/shard_map/while/body/eval_jaxpr/ppermute | solution.py:26
  682.0 8.8 %collective-permute-start.3 = (f32[1,3,512]{2,0,1:T(1,128)S(1)}, f32[1,3,512]{2,0,1:T(1,128)S(1)}, u32[]{:S(2)}, u32[]{:S(2)}) collective-permute-start(f32[1,3,512]{2,0,1:T(1,128)S(1)} %get-tuple-element.810), channel_id=1, source_target_pairs={{0,1},{1,2},{2,3},{3,4},{4,5},{5,6},{6,7},{7,8},{8,9},{9,10},{10,1... | collective-permute-start | bytes 18440 | tf_op jit(solution)/shard_map/while/body/eval_jaxpr/ppermute | solution.py:26
  693.2 8.8 %collective-permute-start.3 = (f32[1,3,512]{2,0,1:T(1,128)S(1)}, f32[1,3,512]{2,0,1:T(1,128)S(1)}, u32[]{:S(2)}, u32[]{:S(2)}) collective-permute-start(f32[1,3,512]{2,0,1:T(1,128)S(1)} %get-tuple-element.810), channel_id=1, source_target_pairs={{0,1},{1,2},{2,3},{3,4},{4,5},{5,6},{6,7},{7,8},{8,9},{9,10},{10,1... | collective-permute-start | bytes 18440 | tf_op jit(solution)/shard_map/while/body/eval_jaxpr/ppermute | solution.py:26
  704.5 8.8 %collective-permute-start.3 = (f32[1,3,512]{2,0,1:T(1,128)S(1)}, f32[1,3,512]{2,0,1:T(1,128)S(1)}, u32[]{:S(2)}, u32[]{:S(2)}) collective-permute-start(f32[1,3,512]{2,0,1:T(1,128)S(1)} %get-tuple-element.810), channel_id=1, source_target_pairs={{0,1},{1,2},{2,3},{3,4},{4,5},{5,6},{6,7},{7,8},{8,9},{9,10},{10,1... | collective-permute-start | bytes 18440 | tf_op jit(solution)/shard_map/while/body/eval_jaxpr/ppermute | solution.py:26
  715.7 8.8 %collective-permute-start.3 = (f32[1,3,512]{2,0,1:T(1,128)S(1)}, f32[1,3,512]{2,0,1:T(1,128)S(1)}, u32[]{:S(2)}, u32[]{:S(2)}) collective-permute-start(f32[1,3,512]{2,0,1:T(1,128)S(1)} %get-tuple-element.810), channel_id=1, source_target_pairs={{0,1},{1,2},{2,3},{3,4},{4,5},{5,6},{6,7},{7,8},{8,9},{9,10},{10,1... | collective-permute-start | bytes 18440 | tf_op jit(solution)/shard_map/while/body/eval_jaxpr/ppermute | solution.py:26
  726.9 8.8 %collective-permute-start.3 = (f32[1,3,512]{2,0,1:T(1,128)S(1)}, f32[1,3,512]{2,0,1:T(1,128)S(1)}, u32[]{:S(2)}, u32[]{:S(2)}) collective-permute-start(f32[1,3,512]{2,0,1:T(1,128)S(1)} %get-tuple-element.810), channel_id=1, source_target_pairs={{0,1},{1,2},{2,3},{3,4},{4,5},{5,6},{6,7},{7,8},{8,9},{9,10},{10,1... | collective-permute-start | bytes 18440 | tf_op jit(solution)/shard_map/while/body/eval_jaxpr/ppermute | solution.py:26
  738.1 8.8 %collective-permute-start.3 = (f32[1,3,512]{2,0,1:T(1,128)S(1)}, f32[1,3,512]{2,0,1:T(1,128)S(1)}, u32[]{:S(2)}, u32[]{:S(2)}) collective-permute-start(f32[1,3,512]{2,0,1:T(1,128)S(1)} %get-tuple-element.810), channel_id=1, source_target_pairs={{0,1},{1,2},{2,3},{3,4},{4,5},{5,6},{6,7},{7,8},{8,9},{9,10},{10,1... | collective-permute-start | bytes 18440 | tf_op jit(solution)/shard_map/while/body/eval_jaxpr/ppermute | solution.py:26
  749.3 8.8 %collective-permute-start.3 = (f32[1,3,512]{2,0,1:T(1,128)S(1)}, f32[1,3,512]{2,0,1:T(1,128)S(1)}, u32[]{:S(2)}, u32[]{:S(2)}) collective-permute-start(f32[1,3,512]{2,0,1:T(1,128)S(1)} %get-tuple-element.810), channel_id=1, source_target_pairs={{0,1},{1,2},{2,3},{3,4},{4,5},{5,6},{6,7},{7,8},{8,9},{9,10},{10,1... | collective-permute-start | bytes 18440 | tf_op jit(solution)/shard_map/while/body/eval_jaxpr/ppermute | solution.py:26
  (143 other events, 2399.1 us)
where the time goes:
time: 770 us; the launch traced here: 760 us
  starting transfers between devices  288 us (37%)
  local copies, waits for them, and re-layouts  155 us (20%)
  matrix products  151 us (20%)
  waiting for transfers between devices  85.6 us (11%)
  other arithmetic  60.5 us (8%)
  blocking collectives  15.2 us (2%)
    unnamed x303, local copies, waits for them, and re-layouts  86.3 us
    unnamed x8, matrix products  83.1 us
    ppermute x21, waiting for transfers between devices, with_halo(): before = lax.ppermute(last, axis, up)  78.9 us
    ppermute x21, starting transfers between devices, with_halo(): before = lax.ppermute(last, axis, up)  71.9 us
    dot_general x20, matrix products, contract(): return jnp.einsum(pattern, left, right, precision=lax.Precision.HIGHEST)  68.1 us
    ppermute x21, starting transfers between devices, with_halo(): after = lax.ppermute(initial, axis, down)  57.5 us
    all_to_all x4, starting transfers between devices, demag_field(): lax.all_to_all(real_part, 'space', split_axis=2, concat_axis=1, tiled=True)  45.5 us
    all_to_all x4, starting transfers between devices, demag_field(): lax.all_to_all(imag_part, 'space', split_axis=2, concat_axis=1, tiled=True)  39.1 us
  transfers between devices with their start and end apart: 58, of which 19 were waited for; matrix products, arithmetic and copies ran while one was open for 20% of the time, Pallas kernels for 0%

commit v1 on v0

v1 whole, which is shorter than its diff:
```python
import math

import jax
import jax.numpy as jnp
import numpy as np
from jax import lax
from jax.experimental import pallas as pl
from jax.experimental.pallas import tpu as pltpu
from jax.sharding import PartitionSpec as P

MESH = pl.DeviceIdType.MESH
F32 = jnp.float32
BF16 = jnp.bfloat16

FINE = 2
step_time = 0.06
damping = 0.02
stiffness = 0.25
thickness = 8.0

GRID = 512
LENGTH = 2 * GRID
ROWS = 16
SPACE = 32
TM = 8
WORKERS = 24
PAIRED = 16


def twiddle_tables():
    unit = 2.0 * np.pi / LENGTH
    col = np.arange(LENGTH)
    wave = 32 * (col // 64) + col % 32
    kind = (col // 32) % 2
    phase = np.where(kind == 1, np.pi / 2, 0.0)
    nyquist = (kind == 1) & (wave == 0)
    wave = np.where(nyquist, GRID, wave)
    phase = np.where(nyquist, 0.0, phase)
    coarse = 16 * np.arange(GRID // 16)[:, None]
    fine = np.arange(16)[:, None]
    angle_coarse = unit * (coarse * wave % LENGTH)
    angle_fine = unit * (fine * wave % LENGTH) + phase
    x = np.arange(GRID)[None, :]
    block = 32 * np.arange(GRID // 32)[:, None]
    inner = np.arange(64)[:, None]
    angle_block = unit * (block * x % LENGTH)
    angle_inner = unit * (inner % 32 * x % LENGTH) + np.where(inner >= 32, np.pi / 2, 0.0)

    def both(angle):
        return np.concatenate([np.cos(angle), np.sin(angle)], axis=0).astype(np.float32)

    return both(angle_coarse), both(angle_fine), both(angle_block), both(angle_inner)


def split(value):
    high = value.astype(BF16)
    return high, (value - high.astype(F32)).astype(BF16)


def dot(left, right):
    return jnp.dot(left, right, preferred_element_type=F32)


def cross(a, b):
    return [
        a[1] * b[2] - a[2] * b[1],
        a[2] * b[0] - a[0] * b[2],
        a[0] * b[1] - a[1] * b[0],
    ]


def torque(magnet, effective):
    first = cross(magnet, effective)
    second = cross(magnet, first)
    scale = -1.0 / (1.0 + damping * damping)
    return [scale * (f + damping * s) for f, s in zip(first, second)]


def kernel(
    state_in, field_in, coupling_in, t_coarse, t_fine, t_block, t_inner, out,
    state, field, coupling, weights, e1_high, e1_low, e2_high, e2_low, diagonal, cross_term,
    outgoing, columns, mixed, answer, returned, edges, edge_in, base, slope, local_field, coarse_end, jumps,
    halo_send, halo_recv, edge_send, edge_recv, out_send, out_recv, back_send, back_recv,
    jump_send, jump_recv, gather_send, gather_recv, forward_send,
):
    slice_index = lax.axis_index("tm")
    place = lax.axis_index("space")
    chip = slice_index // 2
    core = slice_index % 2
    above = (place + SPACE - 1) % SPACE
    below = (place + 1) % SPACE
    offset = (place % 4 - (place // 4) % 4 + 3) % 4
    rank = 3 * (place // 4) + offset
    works = offset < 3
    rank = jnp.minimum(rank, WORKERS - 1)

    def worker_place(worker):
        z = worker // 3
        return 4 * z + (z + 1 + worker % 3) % 4

    barrier = pltpu.get_barrier_semaphore()

    def greet_space(i, carry):
        pl.semaphore_signal(barrier, inc=1, device_id=(slice_index, (place + i) % SPACE), device_id_type=MESH)
        return carry

    def greet_tm(i, carry):
        pl.semaphore_signal(barrier, inc=1, device_id=((slice_index + i) % TM, place), device_id_type=MESH)
        return carry

    lax.fori_loop(1, SPACE, greet_space, 0)
    lax.fori_loop(1, TM, greet_tm, 0)

    zero_rows = jnp.zeros((8, GRID), F32)
    for c in range(3):
        for slot in range(3):
            state[slot, c, 0:8, :] = zero_rows
            state[slot, c, 40:48, :] = zero_rows
        state[2, c, 16:32, :] = state_in[:, c, :]
        field[c, 8:24, :] = field_in[:, c, :]
    coupling[0:8, :] = zero_rows
    coupling[40:48, :] = zero_rows
    coupling[16:32, :] = coupling_in[...]
    edges[...] = zero_rows

    def build_e1(a, carry):
        value = t_coarse[pl.ds(a, 1), :] * t_fine[0:16, :] - t_coarse[pl.ds(32 + a, 1), :] * t_fine[16:32, :]
        high, low = split(value)
        rows = pl.ds(pl.multiple_of(16 * a, 16), 16)
        e1_high[rows, :] = high
        e1_low[rows, :] = low
        return carry

    lax.fori_loop(0, GRID // 16, build_e1, 0)
    inner_row = lax.broadcasted_iota(jnp.int32, (64, GRID), 0)
    inner_lane = lax.broadcasted_iota(jnp.int32, (64, GRID), 1)
    alternating = (1 - 2 * (inner_lane % 2)).astype(F32)

    def build_e2(j, carry):
        value = t_block[pl.ds(j, 1), :] * t_inner[0:64, :] - t_block[pl.ds(16 + j, 1), :] * t_inner[64:128, :]
        value = jnp.where((inner_row == 32) & (j == 0), alternating, value)
        high, low = split(value)
        rows = pl.ds(pl.multiple_of(64 * j, 64), 64)
        e2_high[rows, :] = high
        e2_low[rows, :] = low
        return carry

    lax.fori_loop(0, GRID // 32, build_e2, 0)

    pl.semaphore_wait(barrier, SPACE - 1 + TM - 1)

    def halo_copies():
        copies = []
        for side, target, source_row, landing_row in ((0, below, 24, 8), (1, above, 16, 32)):
            for what, (source, landing) in enumerate(
                (
                    (state.at[2, :, pl.ds(source_row, 8), :], state.at[2, :, pl.ds(landing_row, 8), :]),
                    (field.at[:, pl.ds(source_row - 8, 8), :], field.at[:, pl.ds(landing_row - 8, 8), :]),
                    (coupling.at[pl.ds(source_row, 8), :], coupling.at[pl.ds(landing_row, 8), :]),
                )
            ):
                copies.append(
                    pltpu.make_async_remote_copy(
                        src_ref=source, dst_ref=landing,
                        send_sem=halo_send.at[side, what], recv_sem=halo_recv.at[side, what],
                        device_id=(slice_index, target), device_id_type=MESH,
                    )
                )
        return copies

    first_halo = halo_copies()
    for copy in first_halo:
        copy.start()

    def build_tensor(chunk, carry):
        row = 256 * chunk + lax.broadcasted_iota(jnp.int32, (256, 128), 0)
        lane = lax.broadcasted_iota(jnp.int32, (256, 128), 1)
        quarter = lane // 32
        paired = rank < PAIRED
        wave_y = 32 * (row // 64) + row % 32
        wave_y = jnp.where((wave_y == 0) & ((row // 32) % 2 == 1), GRID, wave_y)
        first_x = jnp.where(paired, 32 * rank, 64 * (rank - PAIRED) + 32 * (quarter // 2))
        wave_x = first_x + lane % 32
        wave_x = jnp.where((wave_x == 0) & (quarter % 2 == 1), GRID, wave_x)
        edge_x = (wave_x == 0) | (wave_x == GRID)
        edge_y = (wave_y == 0) | (wave_y == GRID)
        factor = jnp.where(edge_x, 1.0, 2.0) * jnp.where(edge_y, 1.0, 2.0) * (-1.0 / (LENGTH * LENGTH))
        q_x = wave_x.astype(F32) * (2.0 * math.pi / LENGTH)
        q_y = wave_y.astype(F32) * (2.0 * math.pi / LENGTH)
        squared = q_x * q_x + q_y * q_y
        nonzero = (wave_x + wave_y) > 0
        safe = jnp.where(nonzero, squared, 1.0)
        scaled = jnp.sqrt(safe) * thickness
        film = jnp.where(nonzero, (1.0 - jnp.exp(-scaled)) / scaled, 1.0)
        in_plane = (1.0 - film) / safe
        own_wave = jnp.where(quarter < 2, q_x, q_y)
        diag = jnp.where(paired, in_plane * own_wave * own_wave, film)
        sign = jnp.where(quarter % 2 == 0, -1.0, 1.0)
        mix = jnp.where(edge_x | edge_y | jnp.logical_not(paired), 0.0, sign * in_plane * q_x * q_y)
        diagonal[pl.ds(pl.multiple_of(256 * chunk, 256), 256), :] = diag * factor
        mix = (mix * factor).reshape(4, 2, 32, 128)[:, 0].reshape(128, 128)
        cross_term[pl.ds(pl.multiple_of(128 * chunk, 128), 128), :] = mix
        return carry

    lax.fori_loop(0, 4, build_tensor, 0)

    for copy in first_halo:
        copy.wait()
    coupling[8:16, :] = jnp.where(place > 0, coupling[8:16, :], 0.0)
    coupling[32:40, :] = jnp.where(place < SPACE - 1, coupling[32:40, :], 0.0)

    film_lane = lax.broadcasted_iota(jnp.int32, (8, GRID), 1)
    for g in range(4):
        top = 8 + 8 * g
        mid = coupling[top : top + 8, :]
        scaled = stiffness * mid
        up = scaled * coupling[top - 1 : top + 7, :]
        down = scaled * coupling[top + 1 : top + 9, :]
        left = jnp.where(film_lane == 0, 0.0, scaled * pltpu.roll(mid, 1, 1))
        right = jnp.where(film_lane == GRID - 1, 0.0, scaled * pltpu.roll(mid, GRID - 1, 1))
        rows = slice(8 * g, 8 * g + 8)
        weights[0, rows, :] = up
        weights[1, rows, :] = down
        weights[2, rows, :] = left
        weights[3, rows, :] = right
        weights[4, rows, :] = (up + down) + (left + right)

    def exchange(slot, g):
        top = 8 + 8 * g
        rows = slice(8 * g, 8 * g + 8)
        w = [weights[k, rows, :] for k in range(5)]
        magnet, result = [], []
        for c in range(3):
            mid = state[slot, c, top : top + 8, :]
            total = w[0] * state[slot, c, top - 1 : top + 7, :]
            total = total + w[1] * state[slot, c, top + 1 : top + 9, :]
            total = total + w[2] * pltpu.roll(mid, 1, 1)
            total = total + w[3] * pltpu.roll(mid, GRID - 1, 1)
            magnet.append(mid)
            result.append(total - w[4] * mid)
        return magnet, result

    def coarse_group(slot, g):
        magnet, effective = exchange(slot, g)
        rows = slice(8 * g, 8 * g + 8)
        effective = [effective[c] + field[c, rows, :] for c in range(3)]
        effective[2] = effective[2] - magnet[2]
        rate = torque(magnet, effective)
        return [magnet[c] + (FINE * step_time) * rate[c] for c in range(3)]

    def source_slot(n):
        return jnp.where(n == 0, 2, n % 2)

    def first_sweep(n, carry):
        for g in range(4):
            new = coarse_group(source_slot(n), g)
            for c in range(3):
                state[(n + 1) % 2, c, 8 + 8 * g : 16 + 8 * g, :] = new[c]
        return carry

    lax.fori_loop(0, slice_index, first_sweep, 0)
    start_slot = source_slot(slice_index)
    for g in (1, 2):
        new = coarse_group(start_slot, g)
        for c in range(3):
            coarse_end[c, 8 * g - 8 : 8 * g, :] = new[c]
    for c in range(3):
        start = state[start_slot, c, 16:32, :]
        base[c, :, :] = start
        slope[c, :, :] = jnp.zeros_like(start)
        state[0, c, 16:32, :] = start

    low_half = lax.broadcasted_iota(jnp.int32, (ROWS, 128), 1) < 64
    even_quarter = (lax.broadcasted_iota(jnp.int32, (128, 128), 1) // 32) % 2 == 0

    def partner(value):
        return jnp.where(even_quarter, pltpu.roll(value, 32, 1), pltpu.roll(value, 96, 1))

    def send_column(worker):
        return pltpu.make_async_remote_copy(
            src_ref=outgoing.at[worker],
            dst_ref=columns.at[pl.ds(pl.multiple_of(ROWS * place, ROWS), ROWS), :],
            send_sem=out_send, recv_sem=out_recv,
            device_id=(slice_index, worker_place(worker)), device_id_type=MESH,
        )

    def send_back(target):
        return pltpu.make_async_remote_copy(
            src_ref=answer.at[pl.ds(pl.multiple_of(ROWS * target, ROWS), ROWS), :],
            dst_ref=returned.at[rank],
            send_sem=back_send, recv_sem=back_recv,
            device_id=(slice_index, target), device_id_type=MESH,
        )

    def wait_bytes(ref, semaphore):
        pltpu.make_async_copy(ref, ref, semaphore).wait()

    def evaluation(e, carry):
        slot = e % 2
        for c in range(3):
            edges[c : c + 1, :] = state[0, c, 16:17, :]
            edges[3 + c : 4 + c, :] = state[0, c, 31:32, :]
        edge_copies = [
            pltpu.make_async_remote_copy(
                src_ref=edges, dst_ref=edge_in.at[slot, side],
                send_sem=edge_send.at[side], recv_sem=edge_recv.at[slot, side],
                device_id=(slice_index, target), device_id_type=MESH,
            )
            for side, target in ((0, below), (1, above))
        ]
        for copy in edge_copies:
            copy.start()

        magnet = jnp.concatenate([state[0, c, 16:32, :] for c in range(3)], axis=0)
        high, low = split(magnet)
        stacked = jnp.concatenate([high, low], axis=0)
        for part in range(4):
            cols = slice(256 * part, 256 * part + 256)
            wide = dot(stacked, e1_high[:, cols])
            spectrum = wide[0:48] + wide[48:96] + dot(high, e1_low[:, cols])
            for half in range(2):
                t = 2 * part + half
                lanes = slice(128 * half, 128 * half + 128)
                mx, my, mz = spectrum[0:16, lanes], spectrum[16:32, lanes], spectrum[32:48, lanes]
                outgoing[2 * t] = jnp.where(low_half, mx, pltpu.roll(my, 64, 1))
                outgoing[2 * t + 1] = jnp.where(low_half, pltpu.roll(mx, 64, 1), my)
                outgoing[PAIRED + t] = mz

        def start_column(i, inner):
            worker = (rank + i) % WORKERS

            @pl.when(worker_place(worker) != place)
            def _():
                send_column(worker).start()

            return inner

        lax.fori_loop(0, WORKERS, start_column, 0)

        @pl.when(works)
        def _():
            columns[pl.ds(pl.multiple_of(ROWS * place, ROWS), ROWS), :] = outgoing[rank]

        for copy in edge_copies:
            copy.wait()
        for c in range(3):
            state[0, c, 15:16, :] = edge_in[slot, 0, 3 + c : 4 + c, :]
            state[0, c, 32:33, :] = edge_in[slot, 1, c : c + 1, :]
        for g in (1, 2):
            _, effective = exchange(0, g)
            for c in range(3):
                local_field[c, 8 * g - 8 : 8 * g, :] = effective[c] + field[c, 8 * g : 8 * g + 8, :]

        @pl.when(works)
        def _():
            wait_bytes(columns.at[pl.ds(0, ROWS * (SPACE - 1)), :], out_recv)
            column_high, column_low = split(columns[...])
            column_both = jnp.concatenate([column_high, column_low], axis=1)
            for part in range(4):
                rows = slice(256 * part, 256 * part + 256)
                wide = dot(e2_high[rows, :], column_both)
                spectrum = wide[:, 0:128] + wide[:, 128:256] + dot(e2_low[rows, :], column_high)
                spectrum = spectrum.reshape(4, 2, 32, 128)
                real = spectrum[:, 0].reshape(128, 128)
                imag = spectrum[:, 1].reshape(128, 128)
                diag = diagonal[rows, :].reshape(4, 2, 32, 128)
                mix = cross_term[128 * part : 128 * part + 128, :]
                real_out = diag[:, 0].reshape(128, 128) * real + mix * partner(imag)
                imag_out = diag[:, 1].reshape(128, 128) * imag - mix * partner(real)
                both = jnp.stack(
                    [real_out.reshape(4, 32, 128), imag_out.reshape(4, 32, 128)], axis=1
                ).reshape(256, 128)
                both_high, both_low = split(both)
                mixed[rows, 0:128] = both_high
                mixed[rows, 128:256] = both_low
            for part in range(4):
                rows = slice(128 * part, 128 * part + 128)
                wide = dot(e1_high[rows, :], mixed[...])
                answer[rows, :] = wide[:, 0:128] + wide[:, 128:256] + dot(e1_low[rows, :], mixed[:, 0:128])

                def start_back(i, inner, part=part):
                    target = 8 * part + i

                    @pl.when(target != place)
                    def _():
                        send_back(target).start()

                    return inner

                lax.fori_loop(0, 8, start_back, 0)
            returned[rank] = answer[pl.ds(pl.multiple_of(ROWS * place, ROWS), ROWS), :]
            wait_bytes(outgoing.at[pl.ds(0, WORKERS - 1)], out_send)
            wait_bytes(returned.at[pl.ds(0, WORKERS - 1)], back_recv)

        @pl.when(jnp.logical_not(works))
        def _():
            wait_bytes(outgoing, out_send)
            wait_bytes(returned, back_recv)

        parts = [[], [], []]
        for t in range(8):
            first, second = returned[2 * t], returned[2 * t + 1]
            parts[0].append(jnp.where(low_half, first, pltpu.roll(second, 64, 1)))
            parts[1].append(jnp.where(low_half, pltpu.roll(first, 64, 1), second))
            parts[2].append(returned[PAIRED + t])
        spectrum = jnp.concatenate([jnp.concatenate(part, axis=1) for part in parts], axis=0)
        spectrum_high, spectrum_low = split(spectrum)
        wide = dot(jnp.concatenate([spectrum_high, spectrum_low], axis=0), e2_high[...])
        demag = wide[0:48] + wide[48:96] + dot(spectrum_high, e2_low[...])

        corrects = slot == 1
        length = jnp.where(corrects, 0.5 * step_time, step_time)
        for g in range(2):
            rows = slice(8 * g, 8 * g + 8)
            here = [state[0, c, 16 + 8 * g : 24 + 8 * g, :] for c in range(3)]
            effective = [local_field[c, rows, :] + demag[16 * c + 8 * g : 16 * c + 8 * g + 8] for c in range(3)]
            rate = torque(here, effective)
            for c in range(3):
                start = base[c, rows, :]
                new = start + length * (slope[c, rows, :] + rate[c])
                state[0, c, 16 + 8 * g : 24 + 8 * g, :] = new
                slope[c, rows, :] = jnp.where(corrects, 0.0, rate[c])
                base[c, rows, :] = jnp.where(corrects, new, start)

        @pl.when(works)
        def _():
            wait_bytes(answer.at[pl.ds(0, ROWS * (SPACE - 1)), :], back_send)

        return carry

    lax.fori_loop(0, 2 * FINE, evaluation, 0)

    for c in range(3):
        jumps[slice_index, c, 8:24, :] = state[0, c, 16:32, :] - coarse_end[c, :, :]
    jump_halo = [
        pltpu.make_async_remote_copy(
            src_ref=jumps.at[slice_index, :, pl.ds(source_row, 8), :],
            dst_ref=jumps.at[slice_index, :, pl.ds(landing_row, 8), :],
            send_sem=jump_send.at[side], recv_sem=jump_recv.at[side],
            device_id=(slice_index, target), device_id_type=MESH,
        )
        for side, target, source_row, landing_row in ((0, below, 16, 0), (1, above, 8, 24))
    ]
    for copy in jump_halo:
        copy.start()
    for copy in jump_halo:
        copy.wait()

    def send_jump(n, target, semaphore):
        return pltpu.make_async_remote_copy(
            src_ref=jumps.at[n], dst_ref=jumps.at[n],
            send_sem=semaphore, recv_sem=gather_recv.at[n],
            device_id=(target, place), device_id_type=MESH,
        )

    mate = slice_index + 1 - 2 * core

    @pl.when(core == 0)
    def _():
        send_jump(slice_index, mate, gather_send.at[0]).start()

    for i in (1, 2, 3):

        @pl.when(chip + i < TM // 2)
        def _(i=i):
            send_jump(slice_index, slice_index + 2 * i, gather_send.at[i]).start()

    def second_sweep(n, carry):
        @pl.when(n < slice_index)
        def _():
            wait_bytes(jumps.at[n], gather_recv.at[n])

        @pl.when((n < slice_index) & (n % 2 == core))
        def _():
            send_jump(n, mate, forward_send.at[n]).start()

        for g in range(4):
            new = coarse_group(source_slot(n), g)
            for c in range(3):
                state[(n + 1) % 2, c, 8 + 8 * g : 16 + 8 * g, :] = new[c] + jumps[n, c, 8 * g : 8 * g + 8, :]
        return carry

    lax.fori_loop(0, slice_index + 1, second_sweep, 0)
    for c in range(3):
        out[0, :, c, :] = state[(slice_index + 1) % 2, c, 16:32, :]

    def finish_forward(n, carry):
        @pl.when(n % 2 == core)
        def _():
            wait_bytes(jumps.at[n], forward_send.at[n])

        return carry

    lax.fori_loop(0, slice_index, finish_forward, 0)

    @pl.when(core == 0)
    def _():
        wait_bytes(jumps.at[slice_index], gather_send.at[0])

    for i in (1, 2, 3):

        @pl.when(chip + i < TM // 2)
        def _(i=i):
            wait_bytes(jumps.at[slice_index], gather_send.at[i])


def solution(mesh):
    tables = twiddle_tables()
    vmem = pltpu.VMEM
    dma = pltpu.SemaphoreType.DMA
    scratch = [
        vmem((3, 3, 48, GRID), F32),
        vmem((3, 32, GRID), F32),
        vmem((48, GRID), F32),
        vmem((5, 32, GRID), F32),
        vmem((GRID, LENGTH), BF16),
        vmem((GRID, LENGTH), BF16),
        vmem((LENGTH, GRID), BF16),
        vmem((LENGTH, GRID), BF16),
        vmem((LENGTH, 128), F32),
        vmem((GRID, 128), F32),
        vmem((WORKERS, ROWS, 128), F32),
        vmem((GRID, 128), F32),
        vmem((LENGTH, 256), BF16),
        vmem((GRID, 128), F32),
        vmem((WORKERS, ROWS, 128), F32),
        vmem((8, GRID), F32),
        vmem((2, 2, 8, GRID), F32),
        vmem((3, ROWS, GRID), F32),
        vmem((3, ROWS, GRID), F32),
        vmem((3, ROWS, GRID), F32),
        vmem((3, ROWS, GRID), F32),
        vmem((TM, 3, 32, GRID), F32),
        dma((2, 3)),
        dma((2, 3)),
        dma((2,)),
        dma((2, 2)),
        dma,
        dma,
        dma,
        dma,
        dma((2,)),
        dma((2,)),
        dma((4,)),
        dma((TM,)),
        dma((TM,)),
    ]

    def shards(initial_state, applied_field, coupling):
        return pl.pallas_call(
            kernel,
            out_shape=jax.ShapeDtypeStruct((1, ROWS, 3, GRID), F32),
            in_specs=[pl.BlockSpec(memory_space=pltpu.VMEM)] * 7,
            out_specs=pl.BlockSpec(memory_space=pltpu.VMEM),
            scratch_shapes=scratch,
            compiler_params=pltpu.CompilerParams(collective_id=0, has_side_effects=True),
        )(initial_state, applied_field, coupling, *[jnp.asarray(table) for table in tables])

    return jax.shard_map(
        shards,
        mesh=mesh,
        in_specs=(P("space", None, None), P("space", None, None), P("space", None)),
        out_specs=P("tm", "space", None, None),
        check_vma=False,
    )
```

time: 770 us -> 114 us (0.15)
  the two profiles are of different devices: /device:TPU:128 before, /device:TPU:6 now
where the time goes in v1:
time: 114 us
  Pallas kernels  110 us (96%)
  local copies, waits for them, and re-layouts  3.95 us (3%)
    pallas_call x1, Pallas kernels, shards(): pl.pallas_call(kernel, out_shape=jax.ShapeDtypeStruct((1, ROWS, 3, GRID),...  110 us
    unnamed x4, local copies, waits for them, and re-layouts  2.37 us

profile of v1, /device:TPU:6, one launch (start us, length us, event | category | flops | bytes accessed | tf_op | source)
XLA Modules:
  0.0 113.6 jit_solution(14239605656749491380)
XLA Ops:
  0.0 0.0 copy-start
  0.0 1.6 %copy.8.state_in = f32[16,3,512]{2,1,0:T(4,128)} copy(f32[16,3,512]{2,0,1:T(8,128)} %param.7) | data formatting | bytes 196608 | tf_op args[0]
  1.6 0.0 copy-done
  1.7 0.7 copy.9.field_in
  2.4 109.7 %shard_map.73 = f32[1,16,3,512]{3,2,1,0:T(4,128)} custom-call(f32[16,3,512]{2,1,0:T(4,128)} %copy.8.state_in, f32[16,3,512]{2,1,0:T(4,128)} %copy.9.field_in, f32[16,512]{1,0:T(8,128)} %coupling_in.1, f32[64,1024]{1,0:T(8,128)} %constant.8.clone.t_coarse, f32[32,1024]{1,0:T(8,128)} %constant.9.clone.t_fine, f32[32,512]{1,0:T(8,128)} %constant.10.clone.t_block, ...), custom_call_target="tpu_custom_call" | custom-call | tf_op jit(solution)/shard_map/pallas_call | solution.py:550
  112.1 1.6 %copy.10 = f32[1,16,3,512]{3,1,2,0:T(8,128)} copy(f32[1,16,3,512]{3,2,1,0:T(4,128)} %shard_map.73) | data formatting | bytes 196608 | tf_op jit(solution)/shard_map/pallas_call | solution.py:550
Async XLA Ops:
  0.0 1.7 %copy-start = (f32[16,3,512]{2,0,1:T(8,128)S(1)}, f32[16,3,512]{2,0,1:T(8,128)}, u32[]{:S(2)}) copy-start(f32[16,3,512]{2,0,1:T(8,128)} %param.8) | copy-start | bytes 294916

commit v2 on v1

--- a/solution.py
+++ b/solution.py
@@ -25,6 +25,15 @@
 TM = 8
 WORKERS = 24
 PAIRED = 16
+
+
+def send_order():
+    order = []
+    for far in (4, 3, 2, 1, 0):
+        for dy in (2, 1, -1, 0):
+            for dz in (far, -far) if far in (1, 2, 3) else (far,):
+                order.append((dz, dy if dz >= 0 else -dy))
+    return [pair for pair in order if pair != (0, 0)]
 
 
 def twiddle_tables():
@@ -85,6 +94,10 @@
 ):
     slice_index = lax.axis_index("tm")
     place = lax.axis_index("space")
+
+    def device(which_slice, which_place):
+        return (which_slice, which_place)
+
     chip = slice_index // 2
     core = slice_index % 2
     above = (place + SPACE - 1) % SPACE
@@ -94,18 +107,19 @@
     works = offset < 3
     rank = jnp.minimum(rank, WORKERS - 1)
 
-    def worker_place(worker):
-        z = worker // 3
-        return 4 * z + (z + 1 + worker % 3) % 4
+    place_z, place_y = place // 4, place % 4
+
+    def at(dz, dy):
+        return 4 * ((place_z + dz) % 8) + (place_y + dy) % 4
 
     barrier = pltpu.get_barrier_semaphore()
 
     def greet_space(i, carry):
-        pl.semaphore_signal(barrier, inc=1, device_id=(slice_index, (place + i) % SPACE), device_id_type=MESH)
+        pl.semaphore_signal(barrier, inc=1, device_id=device(slice_index, (place + i) % SPACE), device_id_type=MESH)
         return carry
 
     def greet_tm(i, carry):
-        pl.semaphore_signal(barrier, inc=1, device_id=((slice_index + i) % TM, place), device_id_type=MESH)
+        pl.semaphore_signal(barrier, inc=1, device_id=device((slice_index + i) % TM, place), device_id_type=MESH)
         return carry
 
     lax.fori_loop(1, SPACE, greet_space, 0)
@@ -116,36 +130,12 @@
         for slot in range(3):
             state[slot, c, 0:8, :] = zero_rows
             state[slot, c, 40:48, :] = zero_rows
-        state[2, c, 16:32, :] = state_in[:, c, :]
-        field[c, 8:24, :] = field_in[:, c, :]
+        state[2, c, 16:32, :] = state_in[c]
+        field[c, 8:24, :] = field_in[c]
     coupling[0:8, :] = zero_rows
     coupling[40:48, :] = zero_rows
     coupling[16:32, :] = coupling_in[...]
     edges[...] = zero_rows
-
-    def build_e1(a, carry):
-        value = t_coarse[pl.ds(a, 1), :] * t_fine[0:16, :] - t_coarse[pl.ds(32 + a, 1), :] * t_fine[16:32, :]
-        high, low = split(value)
-        rows = pl.ds(pl.multiple_of(16 * a, 16), 16)
-        e1_high[rows, :] = high
-        e1_low[rows, :] = low
-        return carry
-
-    lax.fori_loop(0, GRID // 16, build_e1, 0)
-    inner_row = lax.broadcasted_iota(jnp.int32, (64, GRID), 0)
-    inner_lane = lax.broadcasted_iota(jnp.int32, (64, GRID), 1)
-    alternating = (1 - 2 * (inner_lane % 2)).astype(F32)
-
-    def build_e2(j, carry):
-        value = t_block[pl.ds(j, 1), :] * t_inner[0:64, :] - t_block[pl.ds(16 + j, 1), :] * t_inner[64:128, :]
-        value = jnp.where((inner_row == 32) & (j == 0), alternating, value)
-        high, low = split(value)
-        rows = pl.ds(pl.multiple_of(64 * j, 64), 64)
-        e2_high[rows, :] = high
-        e2_low[rows, :] = low
-        return carry
-
-    lax.fori_loop(0, GRID // 32, build_e2, 0)
 
     pl.semaphore_wait(barrier, SPACE - 1 + TM - 1)
 
@@ -163,7 +153,7 @@
                     pltpu.make_async_remote_copy(
                         src_ref=source, dst_ref=landing,
                         send_sem=halo_send.at[side, what], recv_sem=halo_recv.at[side, what],
-                        device_id=(slice_index, target), device_id_type=MESH,
+                        device_id=device(slice_index, target), device_id_type=MESH,
                     )
                 )
         return copies
@@ -171,6 +161,30 @@
     first_halo = halo_copies()
     for copy in first_halo:
         copy.start()
+
+    def build_e1(a, carry):
+        value = t_coarse[pl.ds(a, 1), :] * t_fine[0:16, :] - t_coarse[pl.ds(32 + a, 1), :] * t_fine[16:32, :]
+        high, low = split(value)
+        rows = pl.ds(pl.multiple_of(16 * a, 16), 16)
+        e1_high[rows, :] = high
+        e1_low[rows, :] = low
+        return carry
+
+    lax.fori_loop(0, GRID // 16, build_e1, 0)
+    inner_row = lax.broadcasted_iota(jnp.int32, (64, GRID), 0)
+    inner_lane = lax.broadcasted_iota(jnp.int32, (64, GRID), 1)
+    alternating = (1 - 2 * (inner_lane % 2)).astype(F32)
+
+    def build_e2(j, carry):
+        value = t_block[pl.ds(j, 1), :] * t_inner[0:64, :] - t_block[pl.ds(16 + j, 1), :] * t_inner[64:128, :]
+        value = jnp.where((inner_row == 32) & (j == 0), alternating, value)
+        high, low = split(value)
+        rows = pl.ds(pl.multiple_of(64 * j, 64), 64)
+        e2_high[rows, :] = high
+        e2_low[rows, :] = low
+        return carry
+
+    lax.fori_loop(0, GRID // 32, build_e2, 0)
 
     def build_tensor(chunk, carry):
         row = 256 * chunk + lax.broadcasted_iota(jnp.int32, (256, 128), 0)
@@ -276,12 +290,12 @@
     def partner(value):
         return jnp.where(even_quarter, pltpu.roll(value, 32, 1), pltpu.roll(value, 96, 1))
 
-    def send_column(worker):
+    def send_column(worker, target):
         return pltpu.make_async_remote_copy(
             src_ref=outgoing.at[worker],
             dst_ref=columns.at[pl.ds(pl.multiple_of(ROWS * place, ROWS), ROWS), :],
             send_sem=out_send, recv_sem=out_recv,
-            device_id=(slice_index, worker_place(worker)), device_id_type=MESH,
+            device_id=device(slice_index, target), device_id_type=MESH,
         )
 
     def send_back(target):
@@ -289,7 +303,7 @@
             src_ref=answer.at[pl.ds(pl.multiple_of(ROWS * target, ROWS), ROWS), :],
             dst_ref=returned.at[rank],
             send_sem=back_send, recv_sem=back_recv,
-            device_id=(slice_index, target), device_id_type=MESH,
+            device_id=device(slice_index, target), device_id_type=MESH,
         )
 
     def wait_bytes(ref, semaphore):
@@ -304,7 +318,7 @@
             pltpu.make_async_remote_copy(
                 src_ref=edges, dst_ref=edge_in.at[slot, side],
                 send_sem=edge_send.at[side], recv_sem=edge_recv.at[slot, side],
-                device_id=(slice_index, target), device_id_type=MESH,
+                device_id=device(slice_index, target), device_id_type=MESH,
             )
             for side, target in ((0, below), (1, above))
         ]
@@ -326,16 +340,11 @@
                 outgoing[2 * t + 1] = jnp.where(low_half, pltpu.roll(mx, 64, 1), my)
                 outgoing[PAIRED + t] = mz
 
-        def start_column(i, inner):
-            worker = (rank + i) % WORKERS
-
-            @pl.when(worker_place(worker) != place)
-            def _():
-                send_column(worker).start()
-
-            return inner
-
-        lax.fori_loop(0, WORKERS, start_column, 0)
+        for dz, dy in send_order():
+
+            @pl.when((offset + dy - dz) % 4 != 3)
+            def _(dz=dz, dy=dy):
+                send_column(3 * ((place_z + dz) % 8) + (offset + dy - dz) % 4, at(dz, dy)).start()
 
         @pl.when(works)
         def _():
@@ -373,21 +382,24 @@
                 both_high, both_low = split(both)
                 mixed[rows, 0:128] = both_high
                 mixed[rows, 128:256] = both_low
-            for part in range(4):
-                rows = slice(128 * part, 128 * part + 128)
-                wide = dot(e1_high[rows, :], mixed[...])
-                answer[rows, :] = wide[:, 0:128] + wide[:, 128:256] + dot(e1_low[rows, :], mixed[:, 0:128])
-
-                def start_back(i, inner, part=part):
-                    target = 8 * part + i
-
-                    @pl.when(target != place)
-                    def _():
-                        send_back(target).start()
-
-                    return inner
-
-                lax.fori_loop(0, 8, start_back, 0)
+            for parts in ((2,), (1, 3), (0,)):
+                for k in parts:
+                    rows = pl.ds(pl.multiple_of(128 * ((place_z // 2 + k) % 4), 128), 128)
+                    wide = dot(e1_high[rows, :], mixed[...])
+                    answer[rows, :] = wide[:, 0:128] + wide[:, 128:256] + dot(e1_low[rows, :], mixed[:, 0:128])
+                planes = [(k, 1 if k == 1 else 0) for k in parts] + [(k, 0 if k == 1 else 1) for k in parts]
+                for dy in (2, 1, -1, 0):
+                    for k, half in planes:
+                        target = 4 * (2 * ((place_z // 2 + k) % 4) + half) + (place_y + dy) % 4
+                        if k == 0 and dy == 0:
+
+                            @pl.when(target != place)
+                            def _(target=target):
+                                send_back(target).start()
+
+                        else:
+                            send_back(target).start()
+
             returned[rank] = answer[pl.ds(pl.multiple_of(ROWS * place, ROWS), ROWS), :]
             wait_bytes(outgoing.at[pl.ds(0, WORKERS - 1)], out_send)
             wait_bytes(returned.at[pl.ds(0, WORKERS - 1)], back_recv)
@@ -437,7 +449,7 @@
             src_ref=jumps.at[slice_index, :, pl.ds(source_row, 8), :],
             dst_ref=jumps.at[slice_index, :, pl.ds(landing_row, 8), :],
             send_sem=jump_send.at[side], recv_sem=jump_recv.at[side],
-            device_id=(slice_index, target), device_id_type=MESH,
+            device_id=device(slice_index, target), device_id_type=MESH,
         )
         for side, target, source_row, landing_row in ((0, below, 16, 0), (1, above, 8, 24))
     ]
@@ -450,7 +462,7 @@
         return pltpu.make_async_remote_copy(
             src_ref=jumps.at[n], dst_ref=jumps.at[n],
             send_sem=semaphore, recv_sem=gather_recv.at[n],
-            device_id=(target, place), device_id_type=MESH,
+            device_id=device(target, place), device_id_type=MESH,
         )
 
     mate = slice_index + 1 - 2 * core
@@ -482,7 +494,7 @@
 
     lax.fori_loop(0, slice_index + 1, second_sweep, 0)
     for c in range(3):
-        out[0, :, c, :] = state[(slice_index + 1) % 2, c, 16:32, :]
+        out[c] = state[(slice_index + 1) % 2, c, 16:32, :]
 
     def finish_forward(n, carry):
         @pl.when(n % 2 == core)
@@ -547,14 +559,16 @@
     ]
 
     def shards(initial_state, applied_field, coupling):
-        return pl.pallas_call(
+        by_component = [jnp.transpose(value, (1, 0, 2)) for value in (initial_state, applied_field)]
+        result = pl.pallas_call(
             kernel,
-            out_shape=jax.ShapeDtypeStruct((1, ROWS, 3, GRID), F32),
+            out_shape=jax.ShapeDtypeStruct((3, ROWS, GRID), F32),
             in_specs=[pl.BlockSpec(memory_space=pltpu.VMEM)] * 7,
             out_specs=pl.BlockSpec(memory_space=pltpu.VMEM),
             scratch_shapes=scratch,
             compiler_params=pltpu.CompilerParams(collective_id=0, has_side_effects=True),
-        )(initial_state, applied_field, coupling, *[jnp.asarray(table) for table in tables])
+        )(*by_component, coupling, *[jnp.asarray(table) for table in tables])
+        return jnp.transpose(result, (1, 0, 2))[None]
 
     return jax.shard_map(
         shards,

time: 114 us -> 100 us (0.88)
  Pallas kernels: 110 us -> 98.8 us
  local copies, waits for them, and re-layouts: 3.95 us -> 1.54 us
    pallas_call x1, Pallas kernels: 110 us -> 98.8 us  [shards(): pl.pallas_call(kernel, out_shape=jax.ShapeDtypeStruct((3, ROWS, GRID), F3...]
    pallas_call x1 -> x0, local copies, waits for them, and re-layouts: 1.58 us -> none  [shards(): pl.pallas_call(kernel, out_shape=jax.ShapeDtypeStruct((1, ROWS, 3, GRID),...]
    unnamed x4 -> x1, local copies, waits for them, and re-layouts: 2.37 us -> 1.54 us
where the time goes in v2:
time: 100 us
  Pallas kernels  98.8 us (99%)
  local copies, waits for them, and re-layouts  1.54 us (2%)
    pallas_call x1, Pallas kernels, shards(): pl.pallas_call(kernel, out_shape=jax.ShapeDtypeStruct((3, ROWS, GRID), F3...  98.8 us

profile of v2, /device:TPU:6, one launch (start us, length us, event | category | flops | bytes accessed | tf_op | source)
XLA Modules:
  0.0 100.3 jit_solution(3635801587206943994)
XLA Ops:
  0.0 98.8 %shard_map.73 = f32[3,16,512]{2,1,0:T(8,128)} custom-call(f32[3,16,512]{2,1,0:T(8,128)} %bitcast.6, f32[3,16,512]{2,1,0:T(8,128)} %bitcast.7, f32[16,512]{1,0:T(8,128)} %coupling_in.1, f32[64,1024]{1,0:T(8,128)} %constant.8.clone.t_coarse, f32[32,1024]{1,0:T(8,128)} %constant.9.clone.t_fine, f32[32,512]{1,0:T(8,128)} %constant.10.clone.t_block, ...), custom_call_target="tpu_custom_call" | custom-call | tf_op jit(solution)/shard_map/pallas_call | solution.py:563
  98.8 1.5 %copy.9 = f32[1,16,3,512]{3,1,2,0:T(8,128)} copy(f32[1,16,3,512]{3,1,2,0:T(8,128)} %bitcast.5) | data formatting | bytes 196608

commit v3 on v2

--- a/solution.py
+++ b/solution.py
@@ -90,7 +90,7 @@
     state, field, coupling, weights, e1_high, e1_low, e2_high, e2_low, diagonal, cross_term,
     outgoing, columns, mixed, answer, returned, edges, edge_in, base, slope, local_field, coarse_end, jumps,
     halo_send, halo_recv, edge_send, edge_recv, out_send, out_recv, back_send, back_recv,
-    jump_send, jump_recv, gather_send, gather_recv, forward_send,
+    gather_send, gather_recv, rim_send, rim_recv, forward_send, forward_recv,
 ):
     slice_index = lax.axis_index("tm")
     place = lax.axis_index("space")
@@ -442,49 +442,75 @@
 
     lax.fori_loop(0, 2 * FINE, evaluation, 0)
 
+    own = slice_index
+    mate = own + 1 - 2 * core
     for c in range(3):
-        jumps[slice_index, c, 8:24, :] = state[0, c, 16:32, :] - coarse_end[c, :, :]
-    jump_halo = [
-        pltpu.make_async_remote_copy(
-            src_ref=jumps.at[slice_index, :, pl.ds(source_row, 8), :],
-            dst_ref=jumps.at[slice_index, :, pl.ds(landing_row, 8), :],
-            send_sem=jump_send.at[side], recv_sem=jump_recv.at[side],
-            device_id=device(slice_index, target), device_id_type=MESH,
+        jumps[own, c, 8:24, :] = state[0, c, 16:32, :] - coarse_end[c, :, :]
+
+    def send_rows(i):
+        return pltpu.make_async_remote_copy(
+            src_ref=jumps.at[own, :, pl.ds(8, ROWS), :], dst_ref=jumps.at[own, :, pl.ds(8, ROWS), :],
+            send_sem=gather_send.at[i], recv_sem=gather_recv.at[own],
+            device_id=device(own + 2 * i, place), device_id_type=MESH,
         )
-        for side, target, source_row, landing_row in ((0, below, 16, 0), (1, above, 8, 24))
-    ]
-    for copy in jump_halo:
-        copy.start()
-    for copy in jump_halo:
-        copy.wait()
-
-    def send_jump(n, target, semaphore):
+
+    def send_rims(n):
+        return [
+            pltpu.make_async_remote_copy(
+                src_ref=jumps.at[n, :, pl.ds(source_row, 8), :], dst_ref=jumps.at[n, :, pl.ds(landing_row, 8), :],
+                send_sem=rim_send.at[n, side], recv_sem=rim_recv.at[n, side],
+                device_id=device(slice_index, target), device_id_type=MESH,
+            )
+            for side, target, source_row, landing_row in ((0, below, 16, 0), (1, above, 8, 24))
+        ]
+
+    def send_mate(n):
         return pltpu.make_async_remote_copy(
             src_ref=jumps.at[n], dst_ref=jumps.at[n],
-            send_sem=semaphore, recv_sem=gather_recv.at[n],
-            device_id=device(target, place), device_id_type=MESH,
+            send_sem=forward_send.at[n], recv_sem=forward_recv.at[n],
+            device_id=device(mate, place), device_id_type=MESH,
         )
 
-    mate = slice_index + 1 - 2 * core
-
-    @pl.when(core == 0)
-    def _():
-        send_jump(slice_index, mate, gather_send.at[0]).start()
-
-    for i in (1, 2, 3):
+    def holds(i):
+        return core == 0 if i == 0 else chip >= i
+
+    def start_rims(i):
+        @pl.when(holds(i))
+        def _():
+            if i > 0:
+                wait_bytes(jumps.at[own - 2 * i, :, pl.ds(8, ROWS), :], gather_recv.at[own - 2 * i])
+            for copy in send_rims(own - 2 * i):
+                copy.start()
+
+    def pass_on(i):
+        @pl.when(holds(i))
+        def _():
+            for copy in send_rims(own - 2 * i):
+                copy.wait_recv()
+            send_mate(own - 2 * i).start()
+
+    start_rims(0)
+    for i in (2, 3, 1):
 
         @pl.when(chip + i < TM // 2)
         def _(i=i):
-            send_jump(slice_index, slice_index + 2 * i, gather_send.at[i]).start()
+            send_rows(i).start()
+
+    start_rims(1)
+    start_rims(3)
+    start_rims(2)
+    pass_on(0)
+    pass_on(1)
+    pass_on(3)
 
     def second_sweep(n, carry):
-        @pl.when(n < slice_index)
-        def _():
-            wait_bytes(jumps.at[n], gather_recv.at[n])
-
-        @pl.when((n < slice_index) & (n % 2 == core))
-        def _():
-            send_jump(n, mate, forward_send.at[n]).start()
+        @pl.when((chip >= 2) & (n == 2 * chip - 4))
+        def _():
+            pass_on(2)
+
+        @pl.when(n % 2 != core)
+        def _():
+            wait_bytes(jumps.at[n], forward_recv.at[n])
 
         for g in range(4):
             new = coarse_group(source_slot(n), g)
@@ -492,28 +518,25 @@
                 state[(n + 1) % 2, c, 8 + 8 * g : 16 + 8 * g, :] = new[c] + jumps[n, c, 8 * g : 8 * g + 8, :]
         return carry
 
-    lax.fori_loop(0, slice_index + 1, second_sweep, 0)
-    for c in range(3):
-        out[c] = state[(slice_index + 1) % 2, c, 16:32, :]
-
-    def finish_forward(n, carry):
-        @pl.when(n % 2 == core)
-        def _():
-            wait_bytes(jumps.at[n], forward_send.at[n])
-
-        return carry
-
-    lax.fori_loop(0, slice_index, finish_forward, 0)
-
-    @pl.when(core == 0)
-    def _():
-        wait_bytes(jumps.at[slice_index], gather_send.at[0])
-
-    for i in (1, 2, 3):
-
-        @pl.when(chip + i < TM // 2)
+    lax.fori_loop(0, own, second_sweep, 0)
+    for g in (1, 2):
+        new = coarse_group(source_slot(own), g)
+        for c in range(3):
+            out[c, 8 * g - 8 : 8 * g, :] = new[c] + jumps[own, c, 8 * g : 8 * g + 8, :]
+
+    for i in range(4):
+
+        @pl.when(holds(i))
         def _(i=i):
-            wait_bytes(jumps.at[slice_index], gather_send.at[i])
+            for copy in send_rims(own - 2 * i):
+                copy.wait_send()
+            send_mate(own - 2 * i).wait_send()
+
+        if i > 0:
+
+            @pl.when(chip + i < TM // 2)
+            def _(i=i):
+                send_rows(i).wait_send()
 
 
 def solution(mesh):
@@ -551,9 +574,10 @@
         dma,
         dma,
         dma,
-        dma((2,)),
-        dma((2,)),
         dma((4,)),
+        dma((TM,)),
+        dma((TM, 2)),
+        dma((TM, 2)),
         dma((TM,)),
         dma((TM,)),
     ]

time: 100 us -> 96.6 us (0.966)
  Pallas kernels: 98.8 us -> 95 us
    pallas_call x1, Pallas kernels: 98.8 us -> 95 us  [shards(): pl.pallas_call(kernel, out_shape=jax.ShapeDtypeStruct((3, ROWS, GRID), F3...]
where the time goes in v3:
time: 96.6 us; the launch traced here: 96.5 us
  Pallas kernels  95 us (98%)
  local copies, waits for them, and re-layouts  1.54 us (2%)
    pallas_call x1, Pallas kernels, shards(): pl.pallas_call(kernel, out_shape=jax.ShapeDtypeStruct((3, ROWS, GRID), F3...  95 us

profile of v3, /device:TPU:6, one launch (start us, length us, event | category | flops | bytes accessed | tf_op | source)
XLA Modules:
  0.0 96.5 jit_solution(14954088221055098706)
XLA Ops:
  0.0 95.0 %shard_map.73 = f32[3,16,512]{2,1,0:T(8,128)} custom-call(f32[3,16,512]{2,1,0:T(8,128)} %bitcast.6, f32[3,16,512]{2,1,0:T(8,128)} %bitcast.7, f32[16,512]{1,0:T(8,128)} %coupling_in.1, f32[64,1024]{1,0:T(8,128)} %constant.8.clone.t_coarse, f32[32,1024]{1,0:T(8,128)} %constant.9.clone.t_fine, f32[32,512]{1,0:T(8,128)} %constant.10.clone.t_block, ...), custom_call_target="tpu_custom_call" | custom-call | tf_op jit(solution)/shard_map/pallas_call | solution.py:587
  95.0 1.5 %copy.9 = f32[1,16,3,512]{3,1,2,0:T(8,128)} copy(f32[1,16,3,512]{3,1,2,0:T(8,128)} %bitcast.5) | data formatting | bytes 196608

commit v4 on v3

--- a/solution.py
+++ b/solution.py
@@ -25,15 +25,6 @@
 TM = 8
 WORKERS = 24
 PAIRED = 16
-
-
-def send_order():
-    order = []
-    for far in (4, 3, 2, 1, 0):
-        for dy in (2, 1, -1, 0):
-            for dz in (far, -far) if far in (1, 2, 3) else (far,):
-                order.append((dz, dy if dz >= 0 else -dy))
-    return [pair for pair in order if pair != (0, 0)]
 
 
 def twiddle_tables():
@@ -86,10 +77,10 @@
 
 
 def kernel(
-    state_in, field_in, coupling_in, t_coarse, t_fine, t_block, t_inner, out,
-    state, field, coupling, weights, e1_high, e1_low, e2_high, e2_low, diagonal, cross_term,
+    state_in, field_in, coupling_in, coarse_in, fine_in, block_in, inner_in, out,
+    t_coarse, t_fine, t_block, t_inner, state, field, coupling, weights, e1_high, e1_low, e2_high, e2_low, diagonal, cross_term,
     outgoing, columns, mixed, answer, returned, edges, edge_in, base, slope, local_field, coarse_end, jumps,
-    halo_send, halo_recv, edge_send, edge_recv, out_send, out_recv, back_send, back_recv,
+    load, halo_send, halo_recv, edge_send, edge_recv, out_send, out_recv, back_send, back_recv,
     gather_send, gather_recv, rim_send, rim_recv, forward_send, forward_recv,
 ):
     slice_index = lax.axis_index("tm")
@@ -103,14 +94,31 @@
     above = (place + SPACE - 1) % SPACE
     below = (place + 1) % SPACE
     offset = (place % 4 - (place // 4) % 4 + 3) % 4
-    rank = 3 * (place // 4) + offset
     works = offset < 3
-    rank = jnp.minimum(rank, WORKERS - 1)
+
+    def number(plane, turn):
+        return jnp.where(turn < 2, 2 * plane + turn, PAIRED + plane)
+
+    rank = number(place // 4, jnp.minimum(offset, 2))
 
     place_z, place_y = place // 4, place % 4
 
-    def at(dz, dy):
-        return 4 * ((place_z + dz) % 8) + (place_y + dy) % 4
+    loads = [
+        pltpu.make_async_copy(source, landing, load.at[i])
+        for i, (source, landing) in enumerate(
+            (
+                (state_in, state.at[2, :, pl.ds(16, ROWS), :]),
+                (field_in, field.at[:, pl.ds(8, ROWS), :]),
+                (coupling_in, coupling.at[pl.ds(16, ROWS), :]),
+                (coarse_in, t_coarse),
+                (fine_in, t_fine),
+                (block_in, t_block),
+                (inner_in, t_inner),
+            )
+        )
+    ]
+    for copy in loads:
+        copy.start()
 
     barrier = pltpu.get_barrier_semaphore()
 
@@ -130,13 +138,12 @@
         for slot in range(3):
             state[slot, c, 0:8, :] = zero_rows
             state[slot, c, 40:48, :] = zero_rows
-        state[2, c, 16:32, :] = state_in[c]
-        field[c, 8:24, :] = field_in[c]
     coupling[0:8, :] = zero_rows
     coupling[40:48, :] = zero_rows
-    coupling[16:32, :] = coupling_in[...]
     edges[...] = zero_rows
 
+    for copy in loads[:3]:
+        copy.wait()
     pl.semaphore_wait(barrier, SPACE - 1 + TM - 1)
 
     def halo_copies():
@@ -161,6 +168,9 @@
     first_halo = halo_copies()
     for copy in first_halo:
         copy.start()
+
+    for copy in loads[3:]:
+        copy.wait()
 
     def build_e1(a, carry):
         value = t_coarse[pl.ds(a, 1), :] * t_fine[0:16, :] - t_coarse[pl.ds(32 + a, 1), :] * t_fine[16:32, :]
@@ -306,6 +316,9 @@
             device_id=device(slice_index, target), device_id_type=MESH,
         )
 
+    def planes_of(parts):
+        return [(k, 1 if k == 1 else 0) for k in parts] + [(k, 0 if k == 1 else 1) for k in parts]
+
     def wait_bytes(ref, semaphore):
         pltpu.make_async_copy(ref, ref, semaphore).wait()
 
@@ -328,23 +341,30 @@
         magnet = jnp.concatenate([state[0, c, 16:32, :] for c in range(3)], axis=0)
         high, low = split(magnet)
         stacked = jnp.concatenate([high, low], axis=0)
-        for part in range(4):
-            cols = slice(256 * part, 256 * part + 256)
-            wide = dot(stacked, e1_high[:, cols])
-            spectrum = wide[0:48] + wide[48:96] + dot(high, e1_low[:, cols])
-            for half in range(2):
-                t = 2 * part + half
-                lanes = slice(128 * half, 128 * half + 128)
-                mx, my, mz = spectrum[0:16, lanes], spectrum[16:32, lanes], spectrum[32:48, lanes]
-                outgoing[2 * t] = jnp.where(low_half, mx, pltpu.roll(my, 64, 1))
-                outgoing[2 * t + 1] = jnp.where(low_half, pltpu.roll(mx, 64, 1), my)
-                outgoing[PAIRED + t] = mz
-
-        for dz, dy in send_order():
-
-            @pl.when((offset + dy - dz) % 4 != 3)
-            def _(dz=dz, dy=dy):
-                send_column(3 * ((place_z + dz) % 8) + (offset + dy - dz) % 4, at(dz, dy)).start()
+        for parts in ((2, 1, 3, 0),):
+            for k in parts:
+                part = (place_z // 2 + k) % 4
+                cols = pl.ds(pl.multiple_of(256 * part, 256), 256)
+                wide = dot(stacked, e1_high[:, cols])
+                spectrum = wide[0:48] + wide[48:96] + dot(high, e1_low[:, cols])
+                for half in range(2):
+                    t = 2 * part + half
+                    lanes = slice(128 * half, 128 * half + 128)
+                    mx, my, mz = spectrum[0:16, lanes], spectrum[16:32, lanes], spectrum[32:48, lanes]
+                    outgoing[2 * t] = jnp.where(low_half, mx, pltpu.roll(my, 64, 1))
+                    outgoing[2 * t + 1] = jnp.where(low_half, pltpu.roll(mx, 64, 1), my)
+                    outgoing[PAIRED + t] = mz
+        for far in (4, 3, 2, 1, 0):
+            for dy in (2, 1, -1, 0):
+                for dz in (far, -far) if far in (1, 2, 3) else (far,):
+                    sy = dy if dz >= 0 else -dy
+                    if (dz, sy) != (0, 0):
+                        plane = (place_z + dz) % 8
+                        turn = (offset + sy - dz + 8) % 4
+
+                        @pl.when(turn < 3)
+                        def _(plane=plane, turn=turn, sy=sy):
+                            send_column(number(plane, turn), 4 * plane + (place_y + sy) % 4).start()
 
         @pl.when(works)
         def _():
@@ -387,9 +407,8 @@
                     rows = pl.ds(pl.multiple_of(128 * ((place_z // 2 + k) % 4), 128), 128)
                     wide = dot(e1_high[rows, :], mixed[...])
                     answer[rows, :] = wide[:, 0:128] + wide[:, 128:256] + dot(e1_low[rows, :], mixed[:, 0:128])
-                planes = [(k, 1 if k == 1 else 0) for k in parts] + [(k, 0 if k == 1 else 1) for k in parts]
                 for dy in (2, 1, -1, 0):
-                    for k, half in planes:
+                    for k, half in planes_of(parts):
                         target = 4 * (2 * ((place_z // 2 + k) % 4) + half) + (place_y + dy) % 4
                         if k == 0 and dy == 0:
 
@@ -544,6 +563,7 @@
     vmem = pltpu.VMEM
     dma = pltpu.SemaphoreType.DMA
     scratch = [
+        *[vmem(table.shape, F32) for table in tables],
         vmem((3, 3, 48, GRID), F32),
         vmem((3, 32, GRID), F32),
         vmem((48, GRID), F32),
@@ -566,6 +586,7 @@
         vmem((3, ROWS, GRID), F32),
         vmem((3, ROWS, GRID), F32),
         vmem((TM, 3, 32, GRID), F32),
+        dma((7,)),
         dma((2, 3)),
         dma((2, 3)),
         dma((2,)),
@@ -586,8 +607,8 @@
         by_component = [jnp.transpose(value, (1, 0, 2)) for value in (initial_state, applied_field)]
         result = pl.pallas_call(
             kernel,
-            out_shape=jax.ShapeDtypeStruct((3, ROWS, GRID), F32),
-            in_specs=[pl.BlockSpec(memory_space=pltpu.VMEM)] * 7,
+            out_shape=pltpu.VMEM((3, ROWS, GRID), F32),
+            in_specs=[pl.BlockSpec(memory_space=pl.ANY)] * 7,
             out_specs=pl.BlockSpec(memory_space=pltpu.VMEM),
             scratch_shapes=scratch,
             compiler_params=pltpu.CompilerParams(collective_id=0, has_side_effects=True),

time: 96.6 us -> 94.3 us (0.976)
  Pallas kernels: 95 us -> 93.6 us
    pallas_call x1, Pallas kernels: 95 us -> 93.6 us  [shards(): pl.pallas_call(kernel, out_shape=pltpu.VMEM((3, ROWS, GRID), F32), in_spe...]
where the time goes in v4:
time: 94.3 us; the launch traced here: 94.2 us
  Pallas kernels  93.6 us (99%)
    pallas_call x1, Pallas kernels, shards(): pl.pallas_call(kernel, out_shape=pltpu.VMEM((3, ROWS, GRID), F32), in_spe...  93.6 us

profile of v4, /device:TPU:6, one launch (start us, length us, event | category | flops | bytes accessed | tf_op | source)
XLA Modules:
  0.0 94.2 jit_solution(4044340027723569695)
XLA Ops:
  0.0 93.6 %shard_map.73 = f32[3,16,512]{2,1,0:T(8,128)S(1)} custom-call(f32[3,16,512]{2,1,0:T(8,128)} %bitcast.6, f32[3,16,512]{2,1,0:T(8,128)} %bitcast.7, f32[16,512]{1,0:T(8,128)} %coupling_in.1, f32[64,1024]{1,0:T(8,128)} %constant.8.clone.coarse_in, f32[32,1024]{1,0:T(8,128)} %constant.9.clone.fine_in, f32[32,512]{1,0:T(8,128)} %constant.10.clone.block_in, ...), custom_call_target="tpu_custom_call" | custom-call | tf_op jit(solution)/shard_map/pallas_call | solution.py:608
  93.6 0.6 copy.9

commit v5 on v4

--- a/solution.py
+++ b/solution.py
@@ -473,14 +473,15 @@
             device_id=device(own + 2 * i, place), device_id_type=MESH,
         )
 
-    def send_rims(n):
+    def send_rims(i):
+        n, depth = own - 2 * i, 2 * i + 1
         return [
             pltpu.make_async_remote_copy(
-                src_ref=jumps.at[n, :, pl.ds(source_row, 8), :], dst_ref=jumps.at[n, :, pl.ds(landing_row, 8), :],
+                src_ref=jumps.at[n, :, pl.ds(source_row, depth), :], dst_ref=jumps.at[n, :, pl.ds(landing_row, depth), :],
                 send_sem=rim_send.at[n, side], recv_sem=rim_recv.at[n, side],
                 device_id=device(slice_index, target), device_id_type=MESH,
             )
-            for side, target, source_row, landing_row in ((0, below, 16, 0), (1, above, 8, 24))
+            for side, target, source_row, landing_row in ((0, below, 24 - depth, 8 - depth), (1, above, 8, 24))
         ]
 
     def send_mate(n):
@@ -498,13 +499,13 @@
         def _():
             if i > 0:
                 wait_bytes(jumps.at[own - 2 * i, :, pl.ds(8, ROWS), :], gather_recv.at[own - 2 * i])
-            for copy in send_rims(own - 2 * i):
+            for copy in send_rims(i):
                 copy.start()
 
     def pass_on(i):
         @pl.when(holds(i))
         def _():
-            for copy in send_rims(own - 2 * i):
+            for copy in send_rims(i):
                 copy.wait_recv()
             send_mate(own - 2 * i).start()
 
@@ -547,7 +548,7 @@
 
         @pl.when(holds(i))
         def _(i=i):
-            for copy in send_rims(own - 2 * i):
+            for copy in send_rims(i):
                 copy.wait_send()
             send_mate(own - 2 * i).wait_send()
 

time: 94.3 us -> 93.9 us (level)
  no operation moved by 1% of the time
where the time goes in v5:
time: 93.9 us; the launch traced here: 93.8 us
  Pallas kernels  93.2 us (99%)
    pallas_call x1, Pallas kernels, shards(): pl.pallas_call(kernel, out_shape=pltpu.VMEM((3, ROWS, GRID), F32), in_spe...  93.2 us

profile of v5, /device:TPU:6, one launch (start us, length us, event | category | flops | bytes accessed | tf_op | source)
XLA Modules:
  0.0 93.8 jit_solution(4858120288225540775)
XLA Ops:
  0.0 93.2 %shard_map.73 = f32[3,16,512]{2,1,0:T(8,128)S(1)} custom-call(f32[3,16,512]{2,1,0:T(8,128)} %bitcast.6, f32[3,16,512]{2,1,0:T(8,128)} %bitcast.7, f32[16,512]{1,0:T(8,128)} %coupling_in.1, f32[64,1024]{1,0:T(8,128)} %constant.8.clone.coarse_in, f32[32,1024]{1,0:T(8,128)} %constant.9.clone.fine_in, f32[32,512]{1,0:T(8,128)} %constant.10.clone.block_in, ...), custom_call_target="tpu_custom_call" | custom-call | tf_op jit(solution)/shard_map/pallas_call | solution.py:609
  93.2 0.6 copy.9

commit v6 on v5

--- a/solution.py
+++ b/solution.py
@@ -122,8 +122,12 @@
 
     barrier = pltpu.get_barrier_semaphore()
 
+    def far_first(i):
+        step = jnp.where(i % 2 == 0, SPACE - i // 2, (i + 1) // 2)
+        return (place + SPACE // 2 + jnp.where(i == SPACE - 1, 0, step)) % SPACE
+
     def greet_space(i, carry):
-        pl.semaphore_signal(barrier, inc=1, device_id=device(slice_index, (place + i) % SPACE), device_id_type=MESH)
+        pl.semaphore_signal(barrier, inc=1, device_id=device(slice_index, far_first(i)), device_id_type=MESH)
         return carry
 
     def greet_tm(i, carry):
@@ -329,11 +333,11 @@
             edges[3 + c : 4 + c, :] = state[0, c, 31:32, :]
         edge_copies = [
             pltpu.make_async_remote_copy(
-                src_ref=edges, dst_ref=edge_in.at[slot, side],
+                src_ref=edges.at[pl.ds(row, 3), :], dst_ref=edge_in.at[slot, side, pl.ds(row, 3), :],
                 send_sem=edge_send.at[side], recv_sem=edge_recv.at[slot, side],
                 device_id=device(slice_index, target), device_id_type=MESH,
             )
-            for side, target in ((0, below), (1, above))
+            for side, target, row in ((0, below, 3), (1, above, 0))
         ]
         for copy in edge_copies:
             copy.start()

time: 93.9 us -> 93.5 us (level)
  no operation moved by 1% of the time
where the time goes in v6:
time: 93.5 us; the launch traced here: 93.4 us
  Pallas kernels  92.7 us (99%)
    pallas_call x1, Pallas kernels, shards(): pl.pallas_call(kernel, out_shape=pltpu.VMEM((3, ROWS, GRID), F32), in_spe...  92.7 us

profile of v6, /device:TPU:6, one launch (start us, length us, event | category | flops | bytes accessed | tf_op | source)
XLA Modules:
  0.0 93.4 jit_solution(17952632038118666356)
XLA Ops:
  0.0 92.7 %shard_map.73 = f32[3,16,512]{2,1,0:T(8,128)S(1)} custom-call(f32[3,16,512]{2,1,0:T(8,128)} %bitcast.6, f32[3,16,512]{2,1,0:T(8,128)} %bitcast.7, f32[16,512]{1,0:T(8,128)} %coupling_in.1, f32[64,1024]{1,0:T(8,128)} %constant.8.clone.coarse_in, f32[32,1024]{1,0:T(8,128)} %constant.9.clone.fine_in, f32[32,512]{1,0:T(8,128)} %constant.10.clone.block_in, ...), custom_call_target="tpu_custom_call" | custom-call | tf_op jit(solution)/shard_map/pallas_call | solution.py:613
  92.7 0.6 copy.9
